TPU v7x, 32 devices: a whole 2x2x4 slice. The times are simulated.
32 devices in a mesh: ctx: 8 (over z, y), tp: 4 (over x, core).
Axes of the slice: x: 2, y: 2, z: 4, core: 2. Of those that a mesh axis runs over, the one named last changes fastest.
Arguments:
- tokens_in: bfloat16 [4, 2048, 2048], P(None, 'ctx'), may hold values from -6 to 6
- query_weight: bfloat16 [2048, 2048], P('ctx', 'tp'), may hold values from -0.125 to 0.125
- key_weight: bfloat16 [2048, 256], P('ctx', 'tp'), may hold values from -0.125 to 0.125
- value_weight: bfloat16 [2048, 256], P('ctx', 'tp'), may hold values from -0.125 to 0.125
- output_projection_matrix: bfloat16 [2048, 2048], P('tp', 'ctx'), may hold values from -1 to 1
- gate_weight: bfloat16 [2048, 5632], P('ctx', 'tp'), may hold values from -0.125 to 0.125
- up_weight: bfloat16 [2048, 5632], P('ctx', 'tp'), may hold values from -0.125 to 0.125
- down_projection_matrix: bfloat16 [5632, 2048], P('tp', 'ctx'), may hold values from -0.078125 to 0.078125
- gain_attn: bfloat16 [2048], replicated, may hold values from 0.099609375 to 1.8984375
- gain_ffn: bfloat16 [2048], replicated, may hold values from 0.099609375 to 1.8984375
- query_in: bfloat16 [8, 2048, 16], replicated, may hold values from -0.125 to 0.125
- query_out: bfloat16 [8, 16, 2048], P(None, None, 'tp'), may hold values from -0.375 to 0.375
- key_in: bfloat16 [8, 2048, 16], replicated, may hold values from -0.125 to 0.125
- key_out: bfloat16 [8, 16, 256], P(None, None, 'tp'), may hold values from -0.375 to 0.375
- value_in: bfloat16 [8, 2048, 16], replicated, may hold values from -0.125 to 0.125
- value_out: bfloat16 [8, 16, 256], P(None, None, 'tp'), may hold values from -0.375 to 0.375
- output_in: bfloat16 [8, 2048, 16], P(None, 'tp'), may hold values from -1 to 1
- output_adapter_second: bfloat16 [8, 16, 2048], replicated, may hold values from -0.375 to 0.375
- gate_in: bfloat16 [8, 2048, 16], replicated, may hold values from -0.125 to 0.125
- gate_out: bfloat16 [8, 16, 5632], P(None, None, 'tp'), may hold values from -0.375 to 0.375
- up_in: bfloat16 [8, 2048, 16], replicated, may hold values from -0.125 to 0.125
- up_out: bfloat16 [8, 16, 5632], P(None, None, 'tp'), may hold values from -0.375 to 0.375
- down_in: bfloat16 [8, 5632, 16], P(None, 'tp'), may hold values from -0.078125 to 0.078125
- down_adapter_second: bfloat16 [8, 16, 2048], replicated, may hold values from -0.375 to 0.375
- adapter_index: int32 [4], replicated, may hold values from 0 to 7
- cotangent: bfloat16 [4, 2048, 2048], P(None, 'ctx'), may hold values from -6 to 6
Outputs:
- output: bfloat16 [4, 2048, 2048], P(None, 'ctx')
- grad_tokens: bfloat16 [4, 2048, 2048], P(None, 'ctx')
- grad_query_in: float32 [8, 2048, 16], P(None, ('ctx', 'tp'))
- grad_query_out: float32 [8, 16, 2048], P(None, None, 'tp')
- grad_key_in: float32 [8, 2048, 16], P(None, ('ctx', 'tp'))
- grad_key_out: float32 [8, 16, 256], P(None, None, 'tp')
- grad_value_in: float32 [8, 2048, 16], P(None, ('ctx', 'tp'))
- grad_value_out: float32 [8, 16, 256], P(None, None, 'tp')
- grad_output_in: float32 [8, 2048, 16], P(None, 'tp')
- grad_output_out: float32 [8, 16, 2048], replicated
- grad_gate_in: float32 [8, 2048, 16], P(None, ('ctx', 'tp'))
- grad_gate_out: float32 [8, 16, 5632], P(None, None, 'tp')
- grad_up_in: float32 [8, 2048, 16], P(None, ('ctx', 'tp'))
- grad_up_out: float32 [8, 16, 5632], P(None, None, 'tp')
- grad_down_in: float32 [8, 5632, 16], P(None, 'tp')
- grad_down_out: float32 [8, 16, 2048], replicated
All inputs are finite; a program needn't handle non-finite values.
Results may differ from a plain program's by a relative error of at most 0.028.
Values may be sent and summed in bfloat16 or wider, within the bound.
A program may use at most 256 MiB of HBM per device.

v0:
```python
import jax
import jax.numpy as jnp
from jax import lax
from jax.sharding import PartitionSpec as P

HEAD_DIM = 64


eps_norm = 1e-05
theta_base = 10000.0
adapter_scale = 2.0
masked_score = -1e30
highest_precision = lax.Precision.HIGHEST


def norm_forward(values, gain_vector):
    inverse = lax.rsqrt(jnp.mean(values * values, axis=-1, keepdims=True) + eps_norm)
    return (values * inverse * gain_vector, inverse)


def norm_backward(values, gain_vector, inverse, grad_normed):
    weighted = grad_normed * gain_vector
    inner_mean = jnp.mean(weighted * values, axis=-1, keepdims=True)
    return inverse * weighted - values * (inverse * inverse * inverse) * inner_mean


def rotate(values, cosine_part, sine_part):
    half_dim = values.shape[-1] // 2
    first_half = values[..., :half_dim]
    second_half = values[..., half_dim:]
    return jnp.concatenate(
        [
            first_half * cosine_part - second_half * sine_part,
            second_half * cosine_part + first_half * sine_part,
        ],
        axis=-1,
    )


def project(input_tokens, weight_full, selected_input_factor, selected_output_factor):
    frozen_product = jnp.einsum(
        "sbd,do->sbo", input_tokens, weight_full, preferred_element_type=jnp.float32
    )
    reduced_rows = jnp.einsum(
        "ehm,eml->ehl", input_tokens, selected_input_factor, preferred_element_type=jnp.float32
    ).astype(jnp.bfloat16)
    expanded_rows = jnp.einsum(
        "dgi,dip->dgp", reduced_rows, selected_output_factor, preferred_element_type=jnp.float32
    )
    return (frozen_product + adapter_scale * expanded_rows, reduced_rows)


def project_back(
    preactivation_gradient, weight_full, selected_input_factor, selected_output_factor, reduced_rows
):
    reduced_gradient = adapter_scale * jnp.einsum(
        "huk,htk->hut",
        preactivation_gradient,
        selected_output_factor,
        preferred_element_type=jnp.float32,
    )
    grad_inputs = jnp.einsum(
        "sbo,do->sbd", preactivation_gradient, weight_full, preferred_element_type=jnp.float32
    )
    grad_inputs = grad_inputs + jnp.einsum(
        "nao,nko->nak",
        reduced_gradient,
        selected_input_factor.astype(jnp.float32),
        precision=highest_precision,
    )
    second_factor_term = adapter_scale * jnp.einsum(
        "qkm,qke->qme", reduced_rows, preactivation_gradient, preferred_element_type=jnp.float32
    )
    return (grad_inputs, reduced_gradient, second_factor_term)


def per_device(
    tokens_in,
    query_weight,
    key_weight,
    value_weight,
    output_projection_matrix,
    gate_weight,
    up_weight,
    down_projection_matrix,
    gain_attn,
    gain_ffn,
    query_in,
    query_out,
    key_in,
    key_out,
    value_in,
    value_out,
    output_in,
    output_adapter_second,
    gate_in,
    gate_out,
    up_in,
    up_out,
    down_in,
    down_adapter_second,
    adapter_index,
    cotangent,
):
    seq_count = tokens_in.shape[0]
    block_len = tokens_in.shape[1]
    ctx_index = lax.axis_index("ctx")
    total_len = block_len * lax.axis_size("ctx")
    key_block = min(512, total_len)
    score_factor = HEAD_DIM ** (-0.5)
    offsets = jnp.arange(block_len, dtype=jnp.int32)
    query_pos = ctx_index * block_len + offsets
    frequency = theta_base ** (-(jnp.arange(HEAD_DIM // 2).astype(jnp.float32) * 2.0 / HEAD_DIM))
    angles = query_pos.astype(jnp.float32)[:, None] * frequency[None, :]
    cosine_part = jnp.cos(angles)[None, :, None, :]
    sine_part = jnp.sin(angles)[None, :, None, :]
    chooser = (
        adapter_index[:, None] == jnp.arange(query_in.shape[0], dtype=jnp.int32)[None, :]
    ).astype(jnp.bfloat16)
    chooser_wide = chooser.astype(jnp.float32)

    def select(adapter_table):
        return jnp.einsum(
            "sn,nab->sab", chooser, adapter_table, preferred_element_type=jnp.float32
        ).astype(jnp.bfloat16)

    def collect(adapter_term):
        return jnp.einsum("sn,sab->nab", chooser_wide, adapter_term, precision=highest_precision)

    attn_full = (
        lax.all_gather(query_weight, "ctx", axis=0, tiled=True),
        lax.all_gather(key_weight, "ctx", axis=0, tiled=True),
        lax.all_gather(value_weight, "ctx", axis=0, tiled=True),
        lax.all_gather(output_projection_matrix, "ctx", axis=1, tiled=True),
    )
    ffn_full = (
        lax.all_gather(gate_weight, "ctx", axis=0, tiled=True),
        lax.all_gather(up_weight, "ctx", axis=0, tiled=True),
        lax.all_gather(down_projection_matrix, "ctx", axis=1, tiled=True),
    )
    query_full, key_full, value_full, output_full = attn_full
    gate_full, up_full, down_full = ffn_full
    heads_here = query_full.shape[1] // HEAD_DIM
    pair_width = key_full.shape[1]
    pair_heads = pair_width // HEAD_DIM
    group_size = heads_here // pair_heads
    pick_query_in = select(query_in)
    pick_query_out = select(query_out)
    pick_key_in = select(key_in)
    pick_key_out = select(key_out)
    pick_value_in = select(value_in)
    pick_value_out = select(value_out)
    select_output_input = select(output_in)
    output_expansion = select(output_adapter_second)
    pick_gate_in = select(gate_in)
    pick_gate_out = select(gate_out)
    pick_up_in = select(up_in)
    pick_up_out = select(up_out)
    select_down_input = select(down_in)
    down_expansion = select(down_adapter_second)
    tokens = tokens_in.astype(jnp.float32)
    gain_one = gain_attn.astype(jnp.float32)
    gain_two = gain_ffn.astype(jnp.float32)
    normed_wide_one, inverse_one = norm_forward(tokens, gain_one)
    normed_one = normed_wide_one.astype(jnp.bfloat16)
    query_pre, squeeze_query = project(normed_one, query_full, pick_query_in, pick_query_out)
    key_pre, squeeze_key = project(normed_one, key_full, pick_key_in, pick_key_out)
    value_pre, squeeze_value = project(normed_one, value_full, pick_value_in, pick_value_out)
    query_rot = rotate(
        query_pre.reshape(seq_count, block_len, heads_here, HEAD_DIM), cosine_part, sine_part
    ).astype(jnp.bfloat16)
    query_rot = query_rot.reshape(seq_count, block_len, pair_heads, group_size, HEAD_DIM)
    key_rot = rotate(
        key_pre.reshape(seq_count, block_len, pair_heads, HEAD_DIM), cosine_part, sine_part
    ).astype(jnp.bfloat16)
    value_low = value_pre.astype(jnp.bfloat16)
    pair_local = jnp.concatenate(
        [key_rot.reshape(seq_count, block_len, pair_width), value_low], axis=-1
    )
    gathered = lax.all_gather(pair_local, "ctx", axis=1, tiled=True)
    needed = ((ctx_index + 1) * block_len + key_block - 1) // key_block

    def block_scores(pairs_all, block_index):
        key_start = block_index * key_block
        piece_rows = lax.dynamic_slice_in_dim(pairs_all, key_start, key_block, 1)
        keys_part = piece_rows[..., :pair_width].reshape(seq_count, key_block, pair_heads, HEAD_DIM)
        values_part = piece_rows[..., pair_width:].reshape(
            seq_count, key_block, pair_heads, HEAD_DIM
        )
        scores = (
            jnp.einsum(
                "sbkgd,spkd->skgbp", query_rot, keys_part, preferred_element_type=jnp.float32
            )
            * score_factor
        )
        allowed = (key_start + jnp.arange(key_block, dtype=jnp.int32))[None, :] <= query_pos[
            :, None
        ]
        scores = jnp.where(allowed, scores, masked_score)
        return (scores, keys_part, values_part, key_start)

    def forward_block(block_index, carried):
        running_max, running_sum, running_acc = carried
        scores, keys_part, values_part, key_start = block_scores(gathered, block_index)
        new_max = jnp.maximum(running_max, jnp.max(scores, axis=-1))
        weights = jnp.exp(scores - new_max[..., None])
        factor = jnp.exp(running_max - new_max)
        running_sum = running_sum * factor + jnp.sum(weights, axis=-1)
        running_acc = running_acc * factor[..., None] + jnp.einsum(
            "skgbp,spkd->skgbd",
            weights.astype(jnp.bfloat16),
            values_part,
            preferred_element_type=jnp.float32,
        )
        return (new_max, running_sum, running_acc)

    stat_shape = (seq_count, pair_heads, group_size, block_len)
    initial = (
        jnp.full(stat_shape, masked_score, jnp.float32),
        jnp.zeros(stat_shape, jnp.float32),
        jnp.zeros(stat_shape + (HEAD_DIM,), jnp.float32),
    )
    run_max, run_sum, run_acc = lax.fori_loop(0, needed, forward_block, initial)
    log_total = run_max + jnp.log(run_sum)
    mixed_wide = jnp.transpose(run_acc / run_sum[..., None], (0, 3, 1, 2, 4))
    reduced_mixture = mixed_wide.reshape(seq_count, block_len, heads_here * HEAD_DIM).astype(
        jnp.bfloat16
    )
    branch_part = jnp.einsum(
        "sbh,ho->sbo", reduced_mixture, output_full, preferred_element_type=jnp.float32
    )
    squeeze_part = jnp.einsum(
        "uyf,ufa->uya", reduced_mixture, select_output_input, preferred_element_type=jnp.float32
    )
    adapter_branch_total, squeeze_sum = (
        lax.psum(branch_part.astype(jnp.bfloat16), "tp").astype(jnp.float32),
        lax.psum(squeeze_part.astype(jnp.bfloat16), "tp").astype(jnp.float32),
    )
    output_reduction = squeeze_sum.astype(jnp.bfloat16)
    adapter_branch = adapter_branch_total + adapter_scale * jnp.einsum(
        "dgi,dip->dgp", output_reduction, output_expansion, preferred_element_type=jnp.float32
    )
    residual = tokens + adapter_branch
    normed_wide_two, inverse_two = norm_forward(residual, gain_two)
    normed_two = normed_wide_two.astype(jnp.bfloat16)
    gate_pre, squeeze_gate = project(normed_two, gate_full, pick_gate_in, pick_gate_out)
    up_pre, squeeze_up = project(normed_two, up_full, pick_up_in, pick_up_out)
    hidden_state = (jax.nn.silu(gate_pre) * up_pre).astype(jnp.bfloat16)
    ffn_part = jnp.einsum(
        "sbf,fo->sbo", hidden_state, down_full, preferred_element_type=jnp.float32
    )
    down_projection_share = jnp.einsum(
        "dli,diy->dly", hidden_state, select_down_input, preferred_element_type=jnp.float32
    )
    feedforward_total, down_sum = (
        lax.psum(ffn_part.astype(jnp.bfloat16), "tp").astype(jnp.float32),
        lax.psum(down_projection_share.astype(jnp.bfloat16), "tp").astype(jnp.float32),
    )
    down_reduction = down_sum.astype(jnp.bfloat16)
    feedforward_branch = feedforward_total + adapter_scale * jnp.einsum(
        "dgi,dip->dgp", down_reduction, down_expansion, preferred_element_type=jnp.float32
    )
    result = (residual + feedforward_branch).astype(jnp.bfloat16)
    grad_out = cotangent.astype(jnp.float32)
    down_reduction_gradient = (
        adapter_scale
        * jnp.einsum("huk,htk->hut", cotangent, down_expansion, preferred_element_type=jnp.float32)
    ).astype(jnp.bfloat16)
    down_second_term = adapter_scale * jnp.einsum(
        "qkm,qke->qme", down_reduction, cotangent, preferred_element_type=jnp.float32
    )
    term_down_in = jnp.einsum(
        "zvc,zvy->zcy", hidden_state, down_reduction_gradient, preferred_element_type=jnp.float32
    )
    grad_hidden = jnp.einsum(
        "sbo,fo->sbf", cotangent, down_full, preferred_element_type=jnp.float32
    )
    grad_hidden = grad_hidden + jnp.einsum(
        "ugl,uol->ugo",
        down_reduction_gradient,
        select_down_input,
        preferred_element_type=jnp.float32,
    )
    sigmoid = jax.nn.sigmoid(gate_pre)
    grad_gate = (grad_hidden * up_pre * sigmoid * (1.0 + gate_pre * (1.0 - sigmoid))).astype(
        jnp.bfloat16
    )
    grad_up = (grad_hidden * gate_pre * sigmoid).astype(jnp.bfloat16)
    grad_from_gate, gate_reduction_gradient, term_gate_out = project_back(
        grad_gate, gate_full, pick_gate_in, pick_gate_out, squeeze_gate
    )
    grad_from_up, up_reduction_gradient, term_up_out = project_back(
        grad_up, up_full, pick_up_in, pick_up_out, squeeze_up
    )
    grad_normed_two = lax.psum((grad_from_gate + grad_from_up).astype(jnp.bfloat16), "tp").astype(
        jnp.float32
    )
    second_normed_full = normed_two.astype(jnp.float32)
    gate_first_term = jnp.einsum(
        "fyx,fym->fxm", second_normed_full, gate_reduction_gradient, precision=highest_precision
    )
    up_first_term = jnp.einsum(
        "fyx,fym->fxm", second_normed_full, up_reduction_gradient, precision=highest_precision
    )
    grad_residual = grad_out + norm_backward(residual, gain_two, inverse_two, grad_normed_two)
    branch_gradient = grad_residual.astype(jnp.bfloat16)
    output_reduction_gradient = (
        adapter_scale
        * jnp.einsum(
            "huk,htk->hut", branch_gradient, output_expansion, preferred_element_type=jnp.float32
        )
    ).astype(jnp.bfloat16)
    output_second_term = adapter_scale * jnp.einsum(
        "qkm,qke->qme", output_reduction, branch_gradient, preferred_element_type=jnp.float32
    )
    term_output_in = jnp.einsum(
        "mdx,mdy->mxy",
        reduced_mixture,
        output_reduction_gradient,
        preferred_element_type=jnp.float32,
    )
    grad_mixed = jnp.einsum(
        "sbo,ho->sbh", branch_gradient, output_full, preferred_element_type=jnp.float32
    )
    grad_mixed = grad_mixed + jnp.einsum(
        "fvg,fkg->fvk",
        output_reduction_gradient,
        select_output_input,
        preferred_element_type=jnp.float32,
    )
    grad_mixed_grp = grad_mixed.astype(jnp.bfloat16).reshape(
        seq_count, block_len, pair_heads, group_size, HEAD_DIM
    )
    row_delta = jnp.einsum(
        "sbkgd,sbkgd->skgb",
        grad_mixed_grp.astype(jnp.float32),
        mixed_wide,
        precision=highest_precision,
    )

    def backward_block(block_index, carried):
        grad_query, grad_pairs = carried
        scores, keys_part, values_part, key_start = block_scores(gathered, block_index)
        probability = jnp.exp(scores - log_total[..., None])
        grad_values = jnp.einsum(
            "skgbp,sbkgd->spkd",
            probability.astype(jnp.bfloat16),
            grad_mixed_grp,
            preferred_element_type=jnp.float32,
        )
        grad_weights = jnp.einsum(
            "sbkgd,spkd->skgbp", grad_mixed_grp, values_part, preferred_element_type=jnp.float32
        )
        grad_scores = (probability * (grad_weights - row_delta[..., None])).astype(jnp.bfloat16)
        grad_query = grad_query + score_factor * jnp.einsum(
            "skgbp,spkd->sbkgd", grad_scores, keys_part, preferred_element_type=jnp.float32
        )
        grad_keys = score_factor * jnp.einsum(
            "skgbp,sbkgd->spkd", grad_scores, query_rot, preferred_element_type=jnp.float32
        )
        update = jnp.concatenate(
            [
                grad_keys.reshape(seq_count, key_block, pair_width),
                grad_values.reshape(seq_count, key_block, pair_width),
            ],
            axis=-1,
        )
        current = lax.dynamic_slice_in_dim(grad_pairs, key_start, key_block, 1)
        grad_pairs = lax.dynamic_update_slice_in_dim(grad_pairs, current + update, key_start, 1)
        return (grad_query, grad_pairs)

    start_state = (
        jnp.zeros((seq_count, block_len, pair_heads, group_size, HEAD_DIM), jnp.float32),
        jnp.zeros((seq_count, total_len, 2 * pair_width), jnp.float32),
    )
    grad_query, grad_pairs = lax.fori_loop(0, needed, backward_block, start_state)
    grad_pair_local = lax.psum_scatter(
        grad_pairs.astype(jnp.bfloat16), "ctx", scatter_dimension=1, tiled=True
    ).astype(jnp.float32)
    grad_key = rotate(
        grad_pair_local[..., :pair_width].reshape(seq_count, block_len, pair_heads, HEAD_DIM),
        cosine_part,
        -sine_part,
    )
    grad_key = grad_key.reshape(seq_count, block_len, pair_width).astype(jnp.bfloat16)
    grad_value = grad_pair_local[..., pair_width:].astype(jnp.bfloat16)
    grad_query_low = rotate(
        grad_query.reshape(seq_count, block_len, heads_here, HEAD_DIM), cosine_part, -sine_part
    )
    grad_query_low = grad_query_low.reshape(seq_count, block_len, heads_here * HEAD_DIM).astype(
        jnp.bfloat16
    )
    grad_from_query, query_reduction_gradient, term_query_out = project_back(
        grad_query_low, query_full, pick_query_in, pick_query_out, squeeze_query
    )
    grad_from_key, key_reduction_gradient, term_key_out = project_back(
        grad_key, key_full, pick_key_in, pick_key_out, squeeze_key
    )
    grad_from_value, value_reduction_gradient, term_value_out = project_back(
        grad_value, value_full, pick_value_in, pick_value_out, squeeze_value
    )
    grad_normed_terms = grad_from_query + grad_from_key + grad_from_value
    grad_normed_one = lax.psum(grad_normed_terms.astype(jnp.bfloat16), "tp").astype(jnp.float32)
    grad_tokens = (
        grad_residual + norm_backward(tokens, gain_one, inverse_one, grad_normed_one)
    ).astype(jnp.bfloat16)
    first_normed_full = normed_one.astype(jnp.float32)
    term_query_in = jnp.einsum(
        "fyx,fym->fxm", first_normed_full, query_reduction_gradient, precision=highest_precision
    )
    key_first_term = jnp.einsum(
        "fyx,fym->fxm", first_normed_full, key_reduction_gradient, precision=highest_precision
    )
    term_value_in = jnp.einsum(
        "fyx,fym->fxm", first_normed_full, value_reduction_gradient, precision=highest_precision
    )
    all_terms = (
        lax.psum_scatter(collect(term_query_in), ("ctx", "tp"), scatter_dimension=1, tiled=True),
        lax.psum_scatter(collect(key_first_term), ("ctx", "tp"), scatter_dimension=1, tiled=True),
        lax.psum_scatter(collect(term_value_in), ("ctx", "tp"), scatter_dimension=1, tiled=True),
        lax.psum_scatter(collect(gate_first_term), ("ctx", "tp"), scatter_dimension=1, tiled=True),
        lax.psum_scatter(collect(up_first_term), ("ctx", "tp"), scatter_dimension=1, tiled=True),
    )
    ctx_terms = (
        lax.psum(collect(term_query_out).astype(jnp.bfloat16), "ctx").astype(jnp.float32),
        lax.psum(collect(term_key_out).astype(jnp.bfloat16), "ctx").astype(jnp.float32),
        lax.psum(collect(term_value_out).astype(jnp.bfloat16), "ctx").astype(jnp.float32),
        lax.psum(collect(term_output_in).astype(jnp.bfloat16), "ctx").astype(jnp.float32),
        lax.psum(collect(output_second_term).astype(jnp.bfloat16), "ctx").astype(jnp.float32),
        lax.psum(collect(term_gate_out).astype(jnp.bfloat16), "ctx").astype(jnp.float32),
        lax.psum(collect(term_up_out).astype(jnp.bfloat16), "ctx").astype(jnp.float32),
        lax.psum(collect(term_down_in).astype(jnp.bfloat16), "ctx").astype(jnp.float32),
        lax.psum(collect(down_second_term).astype(jnp.bfloat16), "ctx").astype(jnp.float32),
    )
    return (
        result,
        grad_tokens,
        all_terms[0],
        ctx_terms[0],
        all_terms[1],
        ctx_terms[1],
        all_terms[2],
        ctx_terms[2],
        ctx_terms[3],
        ctx_terms[4],
        all_terms[3],
        ctx_terms[5],
        all_terms[4],
        ctx_terms[6],
        ctx_terms[7],
        ctx_terms[8],
    )


def solution(mesh):
    return jax.shard_map(
        per_device,
        mesh=mesh,
        in_specs=(
            P(None, "ctx", None),
            P("ctx", "tp"),
            P("ctx", "tp"),
            P("ctx", "tp"),
            P("tp", "ctx"),
            P("ctx", "tp"),
            P("ctx", "tp"),
            P("tp", "ctx"),
            P(),
            P(),
            P(),
            P(None, None, "tp"),
            P(),
            P(None, None, "tp"),
            P(),
            P(None, None, "tp"),
            P(None, "tp", None),
            P(),
            P(),
            P(None, None, "tp"),
            P(),
            P(None, None, "tp"),
            P(None, "tp", None),
            P(),
            P(),
            P(None, "ctx", None),
        ),
        out_specs=(
            P(None, "ctx", None),
            P(None, "ctx", None),
            P(None, ("ctx", "tp"), None),
            P(None, None, "tp"),
            P(None, ("ctx", "tp"), None),
            P(None, None, "tp"),
            P(None, ("ctx", "tp"), None),
            P(None, None, "tp"),
            P(None, "tp", None),
            P(),
            P(None, ("ctx", "tp"), None),
            P(None, None, "tp"),
            P(None, ("ctx", "tp"), None),
            P(None, None, "tp"),
            P(None, "tp", None),
            P(),
        ),
        check_vma=False,
    )
```

profile of v0, /device:TPU:0, one launch (start us, length us, event | category | flops | bytes accessed | tf_op | source)
XLA Modules:
  0.0 1967.0 jit_solution(11891222879575931494)
XLA Ops:
  12.0 33.6 %all_gather.24 = bf16[2048,64]{0,1:T(8,128)(2,1)S(1)} all-gather(bf16[256,64]{0,1:T(8,128)(2,1)} %param.32), channel_id=1, replica_groups=mesh['ctx'=8,'tp'=4] {'ctx'}, dimensions={0}, use_global_device_ids=true | all-gather | bytes 294912 | tf_op jit(solution)/shard_map/all_gather | solution.py:132
  45.6 31.5 %all_gather.25 = bf16[2048,64]{0,1:T(8,128)(2,1)S(1)} all-gather(bf16[256,64]{0,1:T(8,128)(2,1)} %param.33), channel_id=1, replica_groups=mesh['ctx'=8,'tp'=4] {'ctx'}, dimensions={0}, use_global_device_ids=true | all-gather | bytes 294912 | tf_op jit(solution)/shard_map/all_gather | solution.py:133
  95.3 5.3 fusion.84
  104.8 36.3 %all-gather.7.cloned.1.call-done = bf16[4,2048,128]{1,2,0:T(8,128)(2,1)} async-done(((bf16[4,256,128]{1,2,0:T(8,128)(2,1)}), bf16[4,2048,128]{1,2,0:T(8,128)(2,1)}) %all-gather.7.cloned.1.call-update) | async-done | bytes 2097168 | tf_op jit(solution)/shard_map/all_gather | solution.py:180
  141.4 26.0 %while.28 = (s32[]{:T(128)}, f32[4,1,8,256]{3,2,0,1:T(8,128)S(1)}, f32[4,1,8,256]{3,2,0,1:T(8,128)S(1)}, f32[4,1,8,256,64]{3,4,2,0,1:T(8,128)S(1)}, s32[]{:T(128...) while((s32[]{:T(128)}, f32[4,1,8,256]{3,2,0,1:T(8,128)S(1)}, ...), condition=%wide.region_4.5_spmd.clone, body=%wide.region_1.4_spmd.clone.sunk | while | flops 1121084160 | bytes 57153740 | solution.py:223
  141.6 8.3 fusion.290
  149.9 9.2 fusion.292
  159.2 8.0 bitcast_add_fusion.7
  168.6 23.1 %all-gather.11.cloned.1.call-done = bf16[512,2048]{1,0:T(8,128)(2,1)} async-done(((bf16[512,256]{1,0:T(8,128)(2,1)}), bf16[512,2048]{1,0:T(8,128)(2,1)}) %all-gather.11.cloned.1.call-update) | async-done | bytes 2097168 | tf_op jit(solution)/shard_map/all_gather | solution.py:134
  191.8 6.3 convolution_convert_fusion
  214.5 4.0 fusion.89
  219.3 11.6 psum.106
  230.9 105.6 %all-reduce.8.cloned.1.call-done = bf16[4,256,2048]{2,1,0:T(8,128)(2,1)} async-done(((bf16[4,256,2048]{2,1,0:T(8,128)(2,1)}), bf16[4,256,2048]{2,1,0:T(8,128)(2,1)}) %all-reduce.8.cloned.1.call-update) | async-done | bytes 4194320 | tf_op jit(solution)/shard_map/psum | solution.py:236
  336.5 4.8 multiply_reduce_fusion.1
  348.5 82.5 %all-gather.15.cloned.1.call-done = bf16[2048,1408]{1,0:T(8,128)(2,1)} async-done(((bf16[256,1408]{1,0:T(8,128)(2,1)}), bf16[2048,1408]{1,0:T(8,128)(2,1)}) %all-gather.15.cloned.1.call-update) | async-done | bytes 5767184 | tf_op jit(solution)/shard_map/all_gather | solution.py:138
  431.0 10.4 fusion.69
  445.0 79.3 %all-gather.17.cloned.1.call-done = bf16[1408,2048]{1,0:T(8,128)(2,1)} async-done(((bf16[1408,256]{1,0:T(8,128)(2,1)}), bf16[1408,2048]{1,0:T(8,128)(2,1)}) %all-gather.17.cloned.1.call-update) | async-done | bytes 5767184 | tf_op jit(solution)/shard_map/all_gather | solution.py:139
  524.3 11.0 fusion.63
  538.8 78.2 %all-gather.13.cloned.1.call-done = bf16[2048,1408]{1,0:T(8,128)(2,1)} async-done(((bf16[256,1408]{1,0:T(8,128)(2,1)}), bf16[2048,1408]{1,0:T(8,128)(2,1)}) %all-gather.13.cloned.1.call-update) | async-done | bytes 5767184 | tf_op jit(solution)/shard_map/all_gather | solution.py:137
  617.0 10.6 fusion.73
  627.6 6.7 multiply_convert_fusion.2
  639.6 9.0 fusion.71
  648.6 9.2 fusion.67
  657.8 9.7 add_convert_fusion.1
  668.2 83.1 %all-reduce.10.cloned.1.call-done = bf16[4,256,2048]{2,1,0:T(8,128)(2,1)} async-done(((bf16[4,256,2048]{2,1,0:T(8,128)(2,1)}), bf16[4,256,2048]{2,1,0:T(8,128)(2,1)}) %all-reduce.10.cloned.1.call-update) | async-done | bytes 4194320 | tf_op jit(solution)/shard_map/psum | solution.py:295
  751.3 5.9 multiply_reduce_fusion
  758.4 5.1 fusion.86
  775.3 36.8 %while.29 = (s32[]{:T(128)}, f32[4,256,1,8,64]{1,4,3,0,2:T(8,128)S(1)}, f32[4,2048,128]{1,2,0:T(8,128)}, s32[]{:T(128)}, bf16[4,2048,128]{1,2,0:T(8,128)(2,1)}, ...) while((s32[]{:T(128)}, ...), condition=%wide.region_13.14_spmd.clone, body=%wide.region_12.13_spmd.clone.sunk | while | flops 2728133376 | bytes 91461888 | solution.py:376
  775.5 9.2 fusion.300
  784.6 10.6 fusion.302
  795.3 8.7 fusion.301
  812.1 3.9 convert_element_type.305
  816.0 3.9 fusion.215
  821.0 10.9 copy.288
  831.9 12.6 reshape.335
  844.6 3.9 fusion.216
  849.6 10.9 copy.290
  860.5 12.7 reshape.337
  880.3 10.6 psum.108
  902.5 10.9 copy.282
  913.4 12.8 reshape.329
  936.6 11.0 fusion.75
  947.6 5.6 fusion.82
  953.3 41.3 %reduce-scatter.17.cloned.1.call-done = bf16[4,256,128]{1,2,0:T(8,128)(2,1)} async-done(((bf16[4,2048,128]{1,2,0:T(8,128)(2,1)}), bf16[4,256,128]{1,2,0:T(8,128)(2,1)}) %reduce-scatter.17.cloned.1.call-update) | async-done | bytes 262160 | tf_op jit(solution)/shard_map/reduce_scatter | solution.py:377
  995.6 4.4 fusion.202
  1001.1 10.9 copy.286
  1012.0 12.7 reshape.333
  1025.2 5.7 fusion.133
  1034.3 10.9 copy.284
  1045.2 12.7 reshape.331
  1057.9 5.7 fusion.138
  1063.9 4.6 fusion.118
  1068.5 4.6 fusion.121
  1073.1 17.9 add_convert_fusion
  1091.0 41.4 %reduce-scatter.25.cloned.1.call-done = f32[64,128]{1,0:T(8,128)} async-done(((f32[2048,128]{1,0:T(8,128)}), f32[64,128]{1,0:T(8,128)}) %reduce-scatter.25.cloned.1.call-update) | async-done | bytes 32784
  1134.4 132.7 %reduce-scatter.27.cloned.1.call-done = f32[64,128]{1,0:T(8,128)} async-done(((f32[2048,128]{1,0:T(8,128)}), f32[64,128]{1,0:T(8,128)}) %reduce-scatter.27.cloned.1.call-update) | async-done | bytes 32784
  1269.1 133.2 %reduce-scatter.19.cloned.1.call-done = f32[64,128]{1,0:T(8,128)} async-done(((f32[2048,128]{1,0:T(8,128)}), f32[64,128]{1,0:T(8,128)}) %reduce-scatter.19.cloned.1.call-update) | async-done | bytes 32784
  1404.2 110.3 %all-reduce.12.cloned.1.call-done = (bf16[8,16,512]{2,0,1:T(8,128)(2,1)}, bf16[8,512,16]{1,0,2:T(8,128)(2,1)}, bf16[8,16,2048]{2,0,1:T(8,128)(2,1)}, bf16[8,16,1...) async-done(((bf16[8,16,512]{2,0,1:T(8,128)(2,1)}, bf16[8,512,16]{1,0,2:T(8,128)(2,1)}, ...) | async-done | bytes 2392080 | tf_op jit(solution)/shard_map/psum | solution.py:425
  1528.1 35.7 %all-reduce = (bf16[8,16,64]{2,0,1:T(8,128)(2,1)S(1)}, bf16[8,16,64]{2,0,1:T(8,128)(2,1)S(1)}) all-reduce(bf16[8,16,64]{2,0,1:T(8,128)(2,1)S(1)} %convolution_convert_fusion.22, bf16[8,16,64]{2,0,1:T(8,128)(2,1)S(1)} %convolution_convert_fusion.21), channel_id=1, replica_groups=mesh['ctx'=8,'tp'=4] {'ctx'}, use_global_device_ids=true, to_apply=%region_20.21 | all-reduce | flops 16384 | bytes 65536 | tf_op jit(solution)/shard_map/psum | solution.py:426
  1565.0 87.3 %reduce-scatter.23.cloned.1.call-done = f32[64,128]{1,0:T(8,128)} async-done(((f32[2048,128]{1,0:T(8,128)}), f32[64,128]{1,0:T(8,128)}) %reduce-scatter.23.cloned.1.call-update) | async-done | bytes 32784
  1654.2 132.6 %reduce-scatter.21.cloned.1.call-done = f32[64,128]{1,0:T(8,128)} async-done(((f32[2048,128]{1,0:T(8,128)}), f32[64,128]{1,0:T(8,128)}) %reduce-scatter.21.cloned.1.call-update) | async-done | bytes 32784
  1788.7 150.0 %all-reduce.14.cloned.1.call-done = (bf16[4,256,2048]{2,1,0:T(8,128)(2,1)}, bf16[4,256,2048]{2,1,0:T(8,128)(2,1)}) async-done(((bf16[4,256,2048]{2,1,0:T(8,128)(2,1)}, bf16[4,256,2048]{2,1,0:T(8,128)(2,1)}), (bf16[4,256,2048]{2,1,0:T(8,128)(2,1)}, bf16[4,256,2048]{2,1,0:T(8,128)(2,1)})) %all-reduce.14.cloned.1.call-update) | async-done | bytes 8388624 | tf_op jit(solution)/shard_map/psum | solution.py:256
  1938.7 8.6 add_convert_fusion.2
  1951.2 9.0 fusion.61
  (366 shorter events, 152.0 us)
Async XLA Ops:
  7.2 73.4 %copy-start = (bf16[8,2048,16]{1,2,0:T(8,128)(2,1)S(1)}, bf16[8,2048,16]{1,2,0:T(8,128)(2,1)}, u32[]{:S(2)}) copy-start(bf16[8,2048,16]{1,2,0:T(8,128)(2,1)} %param.44) | copy-start | bytes 1572868
  7.2 88.1 %all-gather.9.cloned.1.call-start = ((), (), s32[]{:S(2)}) async-start(), calls=%async_computation.7 | async-start | bytes 2359296 | tf_op jit(solution)/shard_map/all_gather | solution.py:131
  7.9 133.2 %all-gather.7.cloned.1.call-start = ((), (), s32[]{:S(2)}) async-start(), calls=%async_computation.6 | async-start | bytes 2359296 | tf_op jit(solution)/shard_map/all_gather | solution.py:180
  8.0 73.7 %copy-start.6 = (bf16[4,256,2048]{2,1,0:T(8,128)(2,1)S(1)}, bf16[4,256,2048]{2,1,0:T(8,128)(2,1)}, u32[]{:S(2)}) copy-start(bf16[4,256,2048]{2,1,0:T(8,128)(2,1)} %param.30) | copy-start | bytes 12582916
  11.3 72.0 %copy-start.54 = (bf16[8,2048,16]{1,2,0:T(8,128)(2,1)S(1)}, bf16[8,2048,16]{1,2,0:T(8,128)(2,1)}, u32[]{:S(2)}) copy-start(bf16[8,2048,16]{1,2,0:T(8,128)(2,1)} %param.42) | copy-start | bytes 1572868
  11.3 72.0 %copy-start.59 = (s32[4]{0:T(128)S(1)}, s32[4]{0:T(128)}, u32[]{:S(2)}) copy-start(s32[4]{0:T(128)} %param.54) | copy-start | bytes 52
  12.0 83.3 %copy-start.78 = (f32[2048]{0:T(1024)}, f32[2048]{0:T(1024)S(1)}, u32[]{:S(2)}) copy-start(f32[2048]{0:T(1024)S(1)} %convert_element_type.259) | copy-start | bytes 24580
  45.6 40.2 %copy-start.36 = (bf16[2048,64]{0,1:T(8,128)(2,1)}, bf16[2048,64]{0,1:T(8,128)(2,1)S(1)}, u32[]{:S(2)}) copy-start(bf16[2048,64]{0,1:T(8,128)(2,1)S(1)} %all_gather.24) | copy-start | bytes 786436
  77.1 10.3 copy-start.38
  78.8 16.5 copy-start.92
  80.6 23.8 %copy-start.44 = (f32[256,32]{0,1:T(8,128)}, f32[256,32]{0,1:T(8,128)S(1)}, u32[]{:S(2)}) copy-start(f32[256,32]{0,1:T(8,128)S(1)} %get-tuple-element.290) | copy-start | bytes 98308
  89.7 102.1 %all-gather.11.cloned.1.call-start = ((), (), s32[]{:S(2)}) async-start(), calls=%async_computation.8 | async-start | bytes 2359296 | tf_op jit(solution)/shard_map/all_gather | solution.py:134
  90.4 246.1 %all-reduce.8.cloned.1.call-start = ((), (), s32[]{:S(2)}) async-start(), calls=%async_computation.9 | async-start | bytes 8388608 | tf_op jit(solution)/shard_map/psum | solution.py:236
  91.2 9.4 copy-start.51
  198.1 232.9 %all-gather.15.cloned.1.call-start = ((), (), s32[]{:S(2)}) async-start(), calls=%async_computation.11 | async-start | bytes 6488064 | tf_op jit(solution)/shard_map/all_gather | solution.py:138
  198.7 325.6 %all-gather.17.cloned.1.call-start = ((), (), s32[]{:S(2)}) async-start(), calls=%async_computation.12 | async-start | bytes 6488064 | tf_op jit(solution)/shard_map/all_gather | solution.py:139
  199.3 417.7 %all-gather.13.cloned.1.call-start = ((), (), s32[]{:S(2)}) async-start(), calls=%async_computation.10 | async-start | bytes 6488064 | tf_op jit(solution)/shard_map/all_gather | solution.py:137
  200.0 551.3 %all-reduce.10.cloned.1.call-start = ((), (), s32[]{:S(2)}) async-start(), calls=%async_computation.13 | async-start | bytes 8388608 | tf_op jit(solution)/shard_map/psum | solution.py:295
  200.1 18.4 copy-start.18
  200.1 557.2 %copy-start.68 = (f32[2048]{0:T(1024)}, f32[2048]{0:T(1024)S(1)}, u32[]{:S(2)}) copy-start(f32[2048]{0:T(1024)S(1)} %convert_element_type.280) | copy-start | bytes 24580
  341.4 415.9 %copy-start.80 = (f32[4,256]{1,0:T(4,128)}, f32[4,256]{1,0:T(4,128)S(1)}, u32[]{:S(2)}) copy-start(f32[4,256]{1,0:T(4,128)S(1)} %get-tuple-element.287) | copy-start | bytes 12292
  341.4 415.9 %copy-start.84 = (f32[4,256]{1,0:T(4,128)}, f32[4,256]{1,0:T(4,128)S(1)}, u32[]{:S(2)}) copy-start(f32[4,256]{1,0:T(4,128)S(1)} %get-tuple-element.286) | copy-start | bytes 12292
  431.0 10.5 copy-start.30
  431.0 10.5 copy-start.63
  524.3 11.0 copy-start.28
  524.3 11.0 copy-start.61
  617.0 10.6 copy-start.20
  617.0 10.6 copy-start.46
  617.0 10.6 copy-start.70
  634.3 14.3 copy-start.16
  635.2 22.6 %copy-start.47 = (f32[4,256,16]{1,2,0:T(8,128)}, f32[4,256,16]{1,2,0:T(8,128)S(1)}, u32[]{:S(2)}) copy-start(f32[4,256,16]{1,2,0:T(8,128)S(1)} %convolution_multiply_fusion.10) | copy-start | bytes 196612
  636.0 12.5 copy-start.49
  636.0 12.5 slice-start.2
  648.6 9.2 copy-start.25
  667.5 327.1 %reduce-scatter.17.cloned.1.call-start = ((), (), s32[]{:S(2)}) async-start(), calls=%async_computation.14 | async-start | bytes 2359296 | tf_op jit(solution)/shard_map/reduce_scatter | solution.py:377
  816.0 316.4 %reduce-scatter.25.cloned.1.call-start = ((), (), s32[]{:S(2)}) async-start(), calls=%async_computation.18 | async-start | bytes 1081344
  831.9 12.7 copy-start.48
  844.6 422.5 %reduce-scatter.27.cloned.1.call-start = ((), (), s32[]{:S(2)}) async-start(), calls=%async_computation.19 | async-start | bytes 1081344
  860.5 12.7 copy-start.29
  860.5 15.5 copy-start.71
  873.1 17.7 copy-start.64
  878.8 18.9 copy-start.45
  878.8 523.5 %reduce-scatter.19.cloned.1.call-start = ((), (), s32[]{:S(2)}) async-start(), calls=%async_computation.15 | async-start | bytes 1081344
  913.4 14.3 copy-start.32
  913.4 15.7 copy-start.21
  913.4 17.5 copy-start.19
  913.4 17.5 copy-start.66
  913.4 18.9 copy-start.73
  926.2 588.3 %all-reduce.12.cloned.1.call-start = ((), (), s32[]{:S(2)}) async-start(), calls=%async_computation.20 | async-start | bytes 4784128 | tf_op jit(solution)/shard_map/psum | solution.py:425
  936.3 716.0 %reduce-scatter.23.cloned.1.call-start = ((), (), s32[]{:S(2)}) async-start(), calls=%async_computation.17 | async-start | bytes 1081344
  936.6 11.0 copy-start.98
  947.6 47.0 %copy-start.83 = (bf16[4,16,64]{2,0,1:T(4,128)(2,1)S(1)}, bf16[4,16,64]{2,0,1:T(4,128)(2,1)}, u32[]{:S(2)}) copy-start(bf16[4,16,64]{2,0,1:T(4,128)(2,1)} %copy-done.82) | copy-start | bytes 24580
  1012.0 13.2 copy-start.43
  1024.7 762.1 %reduce-scatter.21.cloned.1.call-start = ((), (), s32[]{:S(2)}) async-start(), calls=%async_computation.16 | async-start | bytes 1081344
  1045.2 12.7 copy-start.41
  1063.7 875.0 %all-reduce.14.cloned.1.call-start = ((), (), s32[]{:S(2)}) async-start(), calls=%async_computation.21 | async-start | bytes 16777216 | tf_op jit(solution)/shard_map/psum | solution.py:256
  1091.0 436.2 %copy-start.89 = (bf16[4,256,16]{1,2,0:T(8,128)(2,1)S(1)}, bf16[4,256,16]{1,2,0:T(8,128)(2,1)}, u32[]{:S(2)}) copy-start(bf16[4,256,16]{1,2,0:T(8,128)(2,1)} %copy-done.88) | copy-start | bytes 98308
  1091.0 436.3 %copy-start.77 = (bf16[4,256,16]{1,2,0:T(8,128)(2,1)S(1)}, bf16[4,256,16]{1,2,0:T(8,128)(2,1)}, u32[]{:S(2)}) copy-start(bf16[4,256,16]{1,2,0:T(8,128)(2,1)} %copy-done.76) | copy-start | bytes 98308
  1269.1 669.7 %copy-start.23 = (bf16[4,16,2048]{2,0,1:T(4,128)(2,1)S(1)}, bf16[4,16,2048]{2,0,1:T(4,128)(2,1)}, u32[]{:S(2)}) copy-start(bf16[4,16,2048]{2,0,1:T(4,128)(2,1)} %copy-done.22) | copy-start | bytes 786436
  1269.1 669.7 %copy-start.58 = (bf16[4,256,16]{1,2,0:T(8,128)(2,1)S(1)}, bf16[4,256,16]{1,2,0:T(8,128)(2,1)}, u32[]{:S(2)}) copy-start(bf16[4,256,16]{1,2,0:T(8,128)(2,1)} %copy-done.57) | copy-start | bytes 98308
  1514.5 11.4 copy-start.53
  1938.7 10.1 slice-start
  1938.7 11.0 slice-start.1
  1951.2 9.1 copy-start.1
  (56 other events, 270.5 us)
Sparse Core Ops, SparseCore 0:
  10.1 55.0 all-gather.8
  89.8 51.3 all-gather.6
  143.2 48.5 all-gather.10
  198.2 138.2 all-reduce.7
  338.5 92.4 all-gather.14
  432.9 91.3 all-gather.16
  526.4 90.4 all-gather.12
  667.6 83.6 all-reduce.9
  816.1 178.4 reduce-scatter.16
  996.7 135.7 reduce-scatter.24
  1134.7 132.3 reduce-scatter.26
  1269.8 132.4 reduce-scatter.18
  1408.0 106.4 all-reduce.11
  1516.6 135.6 reduce-scatter.22
  1654.4 132.3 reduce-scatter.20
  1789.8 148.8 all-reduce.13
where the time goes:
time: 1980 us; the launch traced here: 1970 us
  waiting for transfers between devices  1320 us (67%)
  matrix products  300 us (15%)
  local copies, waits for them, and re-layouts  156 us (8%)
  blocking collectives  123 us (6%)
  other arithmetic  49.5 us (2%)
    unnamed x21, waiting for transfers between devices  531 us
    psum x1, waiting for transfers between devices, per_device(): lax.psum(ffn_part.astype(jnp.bfloat16), 'tp').astype(jnp.float32)  150 us
    unnamed x235, local copies, waits for them, and re-layouts  149 us
    psum x1, waiting for transfers between devices, per_device(): lax.psum(collect(term_query_out).astype(jnp.bfloat16), 'ctx')  110 us
    psum x1, waiting for transfers between devices, per_device(): lax.psum(branch_part.astype(jnp.bfloat16), 'tp').astype(jnp.float32)  106 us
    psum x1, waiting for transfers between devices, per_device(): lax.psum((grad_from_gate + grad_from_up).astype(jnp.bfloat16), 'tp')  83.1 us
    all_gather x1, waiting for transfers between devices, per_device(): lax.all_gather(up_weight, 'ctx', axis=0, tiled=True)  82.5 us
    all_gather x1, waiting for transfers between devices, per_device(): lax.all_gather(down_projection_matrix, 'ctx', axis=1, tiled=True)  79.3 us
  transfers between devices with their start and end apart: 16, of which 15 were waited for; matrix products, arithmetic and copies ran while one was open for 18% of the time, Pallas kernels for 0%

commit v1 on v0

v1 whole, which is shorter than its diff:
```python
import functools

import jax
import jax.numpy as jnp
from jax import lax
from jax.experimental import pallas as pl
from jax.experimental.pallas import tpu as pltpu
from jax.sharding import PartitionSpec as P

HEAD_DIM = 64
LORA = 128

eps_norm = 1e-05
theta_base = 10000.0
adapter_scale = 2.0
masked_score = -1e30
bf16 = jnp.bfloat16
f32 = jnp.float32
MIB = 1024 * 1024


def nn(a, b):
    return lax.dot_general(a, b, (((1,), (0,)), ((), ())), preferred_element_type=f32)


def nt(a, b):
    return lax.dot_general(a, b, (((1,), (1,)), ((), ())), preferred_element_type=f32)


def turn(a):
    return jnp.transpose(a.astype(f32))


def rms(values):
    return lax.rsqrt(jnp.mean(values * values, axis=-1, keepdims=True) + eps_norm)


def norm_backward(values, gain, inverse, grad):
    weighted = grad * gain
    inner = jnp.mean(weighted * values, axis=-1, keepdims=True)
    return inverse * weighted - values * (inverse * inverse * inverse) * inner


def swap_halves(values):
    width = values.shape[-1]
    lane = lax.broadcasted_iota(jnp.int32, values.shape, 1)
    up = pltpu.roll(values, width - HEAD_DIM // 2, 1)
    down = pltpu.roll(values, HEAD_DIM // 2, 1)
    return jnp.where(lane % HEAD_DIM < HEAD_DIM // 2, up, down)


def params(limit=60, **kw):
    return pltpu.CompilerParams(vmem_limit_bytes=limit * MIB, **kw)


def per_seq(*tail):
    zeros = (0,) * len(tail)
    return pl.BlockSpec((None,) + tail, lambda s, *_: (s,) + zeros)


def whole(*shape):
    zeros = (0,) * len(shape)
    return pl.BlockSpec(shape, lambda s, *_: zeros, pipeline_mode=pl.Buffered(1))


def shaped(shape, dtype):
    return jax.ShapeDtypeStruct(shape, dtype)


def qkv_body(t_ref, g_ref, w_ref, a_ref, b_ref, cos_ref, sin_ref, q_ref, kv_ref, xn_ref, s_ref):
    x = t_ref[...].astype(f32)
    xn = (x * rms(x) * g_ref[...]).astype(bf16)
    xn_ref[...] = xn
    s = nn(xn, a_ref[...]).astype(bf16)
    s_ref[...] = s
    pre = nn(xn, w_ref[...]) + nn(s, b_ref[...])
    rot = (pre * cos_ref[...] + swap_halves(pre) * sin_ref[...]).astype(bf16)
    cut = q_ref.shape[-1]
    q_ref[...] = rot[:, :cut]
    kv_ref[...] = rot[:, cut:]


def split_pairs(kv):
    lane = lax.broadcasted_iota(jnp.int32, kv.shape, 1)
    low = lane < HEAD_DIM
    wide = kv.astype(f32)
    swapped = pltpu.roll(wide, HEAD_DIM, 1)
    zero = jnp.zeros_like(wide)
    keys = (jnp.where(low, wide, zero).astype(bf16), jnp.where(low, zero, swapped).astype(bf16))
    vals = (jnp.where(low, swapped, zero).astype(bf16), jnp.where(low, zero, wide).astype(bf16))
    return keys, vals


def attn_fwd_body(c_ref, q_ref, kv_ref, ob_ref, lse_ref, acc_ref, m_ref, l_ref):
    c = c_ref[0]
    rows = q_ref.shape[0]
    heads = q_ref.shape[1] // HEAD_DIM
    m_ref[...] = jnp.full_like(m_ref, masked_score)
    l_ref[...] = jnp.zeros_like(l_ref)
    acc_ref[...] = jnp.zeros_like(acc_ref)

    def block(j, masked):
        kv = kv_ref[j]
        keys, _ = split_pairs(kv)
        v_t = turn(kv)[HEAD_DIM:].astype(bf16)
        if masked:
            kpos = lax.broadcasted_iota(jnp.int32, (rows, rows), 0)
            qpos = lax.broadcasted_iota(jnp.int32, (rows, rows), 1)
            allowed = kpos <= qpos
        for g in range(heads):
            pair = g // 2
            st = nt(keys[g % 2], q_ref[:, pair * 128 : pair * 128 + 128])
            if masked:
                st = jnp.where(allowed, st, masked_score)
            old = m_ref[g : g + 1, :]
            new = jnp.maximum(old, jnp.max(st, axis=0, keepdims=True))
            p = jnp.exp(st - new)
            fade = jnp.exp(old - new)
            m_ref[g : g + 1, :] = new
            l_ref[g : g + 1, :] = l_ref[g : g + 1, :] * fade + jnp.sum(p, axis=0, keepdims=True)
            acc_ref[g] = acc_ref[g] * fade + nn(v_t, p.astype(bf16))

    def step(j, carry):
        block(j, False)
        return carry

    lax.fori_loop(0, c, step, 0)
    block(c, True)
    total = l_ref[...]
    lse_ref[...] = m_ref[...] + jnp.log(total)
    for pair in range(heads // 2):
        top = acc_ref[2 * pair] / total[2 * pair : 2 * pair + 1, :]
        low = acc_ref[2 * pair + 1] / total[2 * pair + 1 : 2 * pair + 2, :]
        both = jnp.concatenate([top, low], axis=0)
        ob_ref[:, pair * 128 : pair * 128 + 128] = turn(both).astype(bf16)


def attn_bwd_body(
    c_ref, q_ref, kv_ref, do_ref, ob_ref, lse_ref, cos_ref, sin_ref, dq_ref, dkv_ref, dqt_ref, dl_ref
):
    c = c_ref[0]
    rows = q_ref.shape[0]
    heads = q_ref.shape[1] // HEAD_DIM
    dqt_ref[...] = jnp.zeros_like(dqt_ref)
    for pair in range(heads // 2):
        cols = slice(pair * 128, pair * 128 + 128)
        prod = turn(do_ref[:, cols].astype(f32) * ob_ref[:, cols].astype(f32))
        dl_ref[2 * pair : 2 * pair + 1, :] = jnp.sum(prod[:HEAD_DIM], axis=0, keepdims=True)
        dl_ref[2 * pair + 1 : 2 * pair + 2, :] = jnp.sum(prod[HEAD_DIM:], axis=0, keepdims=True)

    def block(j, masked):
        kv = kv_ref[j]
        keys, vals = split_pairs(kv)
        k_t = turn(kv)[:HEAD_DIM].astype(bf16)
        if masked:
            kpos = lax.broadcasted_iota(jnp.int32, (rows, rows), 0)
            qpos = lax.broadcasted_iota(jnp.int32, (rows, rows), 1)
            allowed = kpos <= qpos
        dk = [None, None]
        dv = [None, None]
        for g in range(heads):
            pair = g // 2
            cols = slice(pair * 128, pair * 128 + 128)
            q2 = q_ref[:, cols]
            do2 = do_ref[:, cols]
            st = nt(keys[g % 2], q2)
            p = jnp.exp(st - lse_ref[g : g + 1, :])
            if masked:
                p = jnp.where(allowed, p, 0.0)
            dp = nt(vals[g % 2], do2)
            ds = (p * (dp - dl_ref[g : g + 1, :])).astype(bf16)
            v_part = nn(p.astype(bf16), do2)
            k_part = nn(ds, q2)
            dk[g % 2] = k_part if dk[g % 2] is None else dk[g % 2] + k_part
            dv[g % 2] = v_part if dv[g % 2] is None else dv[g % 2] + v_part
            dqt_ref[g] = dqt_ref[g] + nn(k_t, ds)
        lane = lax.broadcasted_iota(jnp.int32, kv.shape, 1)
        dkeys = dk[0] + pltpu.roll(dk[1], HEAD_DIM, 1)
        dvals = dv[1] + pltpu.roll(dv[0], HEAD_DIM, 1)
        dkv_ref[j] = jnp.where(lane < HEAD_DIM, dkeys, dvals).astype(bf16)

    def step(j, carry):
        block(j, False)
        return carry

    lax.fori_loop(0, c, step, 0)
    block(c, True)

    def clear(j, carry):
        dkv_ref[j] = jnp.zeros(dkv_ref.shape[1:], bf16)
        return carry

    lax.fori_loop(c + 1, dkv_ref.shape[0], clear, 0)
    for pair in range(heads // 2):
        both = jnp.concatenate([dqt_ref[2 * pair], dqt_ref[2 * pair + 1]], axis=0)
        wide = turn(both)
        dq = wide * cos_ref[...] - swap_halves(wide) * sin_ref[...]
        dq_ref[:, pair * 128 : pair * 128 + 128] = dq.astype(bf16)


def mix_body(ob_ref, w_ref, a_ref, out_ref):
    ob = ob_ref[...]
    cut = w_ref.shape[-1]
    out_ref[:, :cut] = nn(ob, w_ref[...]).astype(bf16)
    out_ref[:, cut:] = nn(ob, a_ref[...]).astype(bf16)


def residual_of(t_ref, z_ref, bo_ref):
    width = t_ref.shape[-1]
    so = z_ref[:, width:]
    return t_ref[...].astype(f32) + (z_ref[:, :width].astype(f32) + nn(so, bo_ref[...])), so


def ffn_body(
    t_ref, z_ref, bo_ref, g_ref, agu_ref, wg_ref, wu_ref, bg_ref, bu_ref, wd_ref, ad_ref, bd_ref, dy_ref,
    p2_ref, p3_ref, dbg_ref, dbu_ref, dad_ref,
):
    width = t_ref.shape[-1]
    h, _ = residual_of(t_ref, z_ref, bo_ref)
    xn = (h * rms(h) * g_ref[...]).astype(bf16)
    s = nn(xn, agu_ref[...]).astype(bf16)
    gate = nn(xn, wg_ref[...]) + nn(s, bg_ref[...])
    up = nn(xn, wu_ref[...]) + nn(s, bu_ref[...])
    sig = jax.nn.sigmoid(gate)
    hidden = (gate * sig * up).astype(bf16)
    dy = dy_ref[...]
    dsd = nt(dy, bd_ref[...]).astype(bf16)
    dhid = nt(dy, wd_ref[...]) + nt(dsd, ad_ref[...])
    dgate = (dhid * up * sig * (1.0 + gate * (1.0 - sig))).astype(bf16)
    dup = (dhid * gate * sig).astype(bf16)
    p3_ref[:, :width] = nn(hidden, wd_ref[...]).astype(bf16)
    p3_ref[:, width:] = nn(hidden, ad_ref[...]).astype(bf16)
    p2_ref[:, :width] = (nt(dgate, wg_ref[...]) + nt(dup, wu_ref[...])).astype(bf16)
    p2_ref[:, width:] = (nt(dgate, bg_ref[...]) + nt(dup, bu_ref[...])).astype(bf16)
    s_t = turn(s).astype(bf16)
    rank = dbg_ref.shape[0]
    dbg_ref[...] = (adapter_scale * nn(s_t, dgate)[:rank]).astype(bf16)
    dbu_ref[...] = (adapter_scale * nn(s_t, dup)[rank : 2 * rank]).astype(bf16)
    dad_ref[...] = nn(turn(dsd).astype(bf16), hidden)[:rank].astype(bf16)


def back_body(
    t_ref, z_ref, bo_ref, g_ref, agu_ref, p2_ref, dy_ref, w_ref, ao_ref, ob_ref,
    dh_ref, dob_ref, dbo_ref, dao_ref, dgu_ref,
):
    width = t_ref.shape[-1]
    h, so = residual_of(t_ref, z_ref, bo_ref)
    inverse = rms(h)
    gain = g_ref[...]
    xn = (h * inverse * gain).astype(bf16)
    ds = p2_ref[:, width:]
    dxn = p2_ref[:, :width].astype(f32) + nt(ds, agu_ref[...])
    dh = dy_ref[...].astype(f32) + norm_backward(h, gain, inverse, dxn)
    dz = dh.astype(bf16)
    dh_ref[...] = dz
    dso = nt(dz, bo_ref[...]).astype(bf16)
    dob_ref[...] = (nt(dz, w_ref[...]) + nt(dso, ao_ref[...])).astype(bf16)
    rank = dbo_ref.shape[0]
    dbo_ref[...] = (adapter_scale * nn(turn(so).astype(bf16), dz)[:rank]).astype(bf16)
    dao_ref[...] = nn(turn(dso).astype(bf16), ob_ref[...])[:rank].astype(bf16)
    dgu_ref[...] = nn(turn(ds).astype(bf16), xn)[: 2 * rank].astype(bf16)


def result_body(t_ref, z_ref, bo_ref, p3_ref, bd_ref, dy_ref, out_ref, dbd_ref):
    width = t_ref.shape[-1]
    h, _ = residual_of(t_ref, z_ref, bo_ref)
    sd = p3_ref[:, width:]
    out_ref[...] = (h + (p3_ref[:, :width].astype(f32) + nn(sd, bd_ref[...]))).astype(bf16)
    rank = dbd_ref.shape[0]
    dbd_ref[...] = (adapter_scale * nn(turn(sd).astype(bf16), dy_ref[...])[:rank]).astype(bf16)


def dqkv_body(dq_ref, dkv_ref, cos_ref, sin_ref, w_ref, b_ref, s_ref, p4_ref, db_ref):
    width = w_ref.shape[0]
    dkv = dkv_ref[...]
    back = (dkv * cos_ref[...] - swap_halves(dkv) * sin_ref[...]).astype(bf16)
    both = jnp.concatenate([dq_ref[...], back], axis=1)
    p4_ref[:, :width] = nt(both, w_ref[...]).astype(bf16)
    p4_ref[:, width:] = nt(both, b_ref[...]).astype(bf16)
    db_ref[...] = (adapter_scale * nn(turn(s_ref[...]).astype(bf16), both)[: db_ref.shape[0]]).astype(bf16)


def last_body(t_ref, g_ref, xn_ref, p4_ref, a_ref, dh_ref, out_ref, da_ref):
    width = t_ref.shape[-1]
    x = t_ref[...].astype(f32)
    ds = p4_ref[:, width:]
    dxn = p4_ref[:, :width].astype(f32) + nt(ds, a_ref[...])
    out_ref[...] = (dh_ref[...].astype(f32) + norm_backward(x, g_ref[...], rms(x), dxn)).astype(bf16)
    da_ref[...] = nn(turn(ds).astype(bf16), xn_ref[...])[: da_ref.shape[0]].astype(bf16)


def greet(peers):
    barrier = pltpu.get_barrier_semaphore()
    for peer in peers:
        pl.semaphore_signal(barrier, inc=1, device_id=peer, device_id_type=pl.DeviceIdType.MESH)
    pl.semaphore_wait(barrier, len(peers))


def ring_place(index, n):
    return jnp.where(index % 2 == 0, index // 2, n - 1 - index // 2)


def ring_index(place, n):
    place = lax.rem(place + 2 * n, n)
    return jnp.where(place < n // 2, 2 * place, 2 * (n - 1 - place) + 1)


def remote(src, dst, send, recv, peer):
    return pltpu.make_async_remote_copy(
        src_ref=src, dst_ref=dst, send_sem=send, recv_sem=recv, device_id=peer,
        device_id_type=pl.DeviceIdType.MESH,
    )


def ring_gather_body(n, in_ref, out_ref, send, recv, local):
    me = lax.axis_index("ctx")
    place = ring_place(me, n)
    right = {"ctx": ring_index(place + 1, n)}
    left = {"ctx": ring_index(place - 1, n)}
    greet((left, right))
    mine = pltpu.make_async_copy(in_ref, out_ref.at[me], local)
    mine.start()
    steps = n // 2
    half = in_ref.shape[0] // 2
    for k in range(steps):
        last = k == steps - 1
        copies = []
        for way, peer in ((0, right), (1, left)):
            owner = me if k == 0 else ring_index(place + (k if way else -k), n)
            part = pl.ds(way * half, half) if last else pl.ds(0, 2 * half)
            src = in_ref.at[part] if k == 0 else out_ref.at[owner, part]
            copies.append(
                remote(src, out_ref.at[owner, part], send.at[way, k], recv.at[way, k], peer)
            )
        for copy in copies:
            copy.start()
        for copy in copies:
            copy.wait()
    mine.wait()


def ring_gather(block, n, collective_id):
    return pl.pallas_call(
        functools.partial(ring_gather_body, n),
        out_shape=shaped((n,) + block.shape, block.dtype),
        in_specs=[pl.BlockSpec(memory_space=pltpu.VMEM)],
        out_specs=pl.BlockSpec(memory_space=pltpu.VMEM),
        scratch_shapes=[
            pltpu.SemaphoreType.DMA((2, n // 2)),
            pltpu.SemaphoreType.DMA((2, n // 2)),
            pltpu.SemaphoreType.DMA,
        ],
        compiler_params=params(collective_id=collective_id, has_side_effects=True),
    )(block)


def ring_scatter_body(n, in_ref, out_ref, got, held, send, recv):
    me = lax.axis_index("ctx")
    place = ring_place(me, n)
    right = {"ctx": ring_index(place + 1, n)}
    left = {"ctx": ring_index(place - 1, n)}
    greet((left, right))
    steps = n // 2
    half = in_ref.shape[1] // 2
    for k in range(steps):
        copies = []
        for way, peer in ((0, right), (1, left)):
            ahead = steps - k
            dest = ring_index(place + (-ahead if way else ahead), n)
            mine = pl.ds(way * half, half)
            if k == 0:
                src = in_ref.at[dest, mine]
                dst = got.at[way, 0, mine]
            else:
                if k == 1:
                    rest = pl.ds((1 - way) * half, half)
                    held[way, 1, mine] = (
                        in_ref[dest, mine].astype(f32) + got[way, 0, mine].astype(f32)
                    ).astype(bf16)
                    held[way, 1, rest] = in_ref[dest, rest]
                else:
                    held[way, k] = (
                        in_ref[dest].astype(f32) + got[way, k - 1].astype(f32)
                    ).astype(bf16)
                src = held.at[way, k]
                dst = got.at[way, k]
            copies.append(remote(src, dst, send.at[way, k], recv.at[way, k], peer))
        for copy in copies:
            copy.start()
        for copy in copies:
            copy.wait()
    out_ref[...] = (
        in_ref[me].astype(f32) + got[0, steps - 1].astype(f32) + got[1, steps - 1].astype(f32)
    )


def ring_scatter(blocks, n, collective_id):
    tail = blocks.shape[1:]
    return pl.pallas_call(
        functools.partial(ring_scatter_body, n),
        out_shape=shaped(tail, f32),
        in_specs=[pl.BlockSpec(memory_space=pltpu.VMEM)],
        out_specs=pl.BlockSpec(memory_space=pltpu.VMEM),
        scratch_shapes=[
            pltpu.VMEM((2, n // 2) + tail, blocks.dtype),
            pltpu.VMEM((2, n // 2) + tail, blocks.dtype),
            pltpu.SemaphoreType.DMA((2, n // 2)),
            pltpu.SemaphoreType.DMA((2, n // 2)),
        ],
        compiler_params=params(collective_id=collective_id, has_side_effects=True),
    )(blocks)


def tp_sum_body(chunks, in_ref, out_ref, near, far, mid, send, recv):
    me = lax.axis_index("tp")
    core = lax.rem(me, 2)
    other_core = {"tp": me + 1 - 2 * core}
    other_chip = {"tp": lax.rem(me + 2, 4)}
    greet((other_core, other_chip))
    half = in_ref.shape[0] // chunks // 2

    def rows(i, which):
        return pl.ds(pl.multiple_of((2 * i + which) * half, half), half)

    firsts, seconds, thirds = [], [], []
    for i in range(chunks):
        copy = remote(in_ref.at[rows(i, 1 - core)], near.at[i], send.at[0, i], recv.at[0, i], other_core)
        copy.start()
        firsts.append(copy)
    for i in range(chunks):
        firsts[i].wait_recv()
        mid[i] = (in_ref[rows(i, core), :].astype(f32) + near[i].astype(f32)).astype(bf16)
        copy = remote(mid.at[i], far.at[i], send.at[1, i], recv.at[1, i], other_chip)
        copy.start()
        seconds.append(copy)
    for i in range(chunks):
        seconds[i].wait_recv()
        out_ref[rows(i, core), :] = (mid[i].astype(f32) + far[i].astype(f32)).astype(bf16)
        span = rows(i, core)
        copy = remote(out_ref.at[span], out_ref.at[span], send.at[2, i], recv.at[2, i], other_core)
        copy.start()
        thirds.append(copy)
    for i in range(chunks):
        thirds[i].wait_recv()
        firsts[i].wait_send()
        seconds[i].wait_send()
        thirds[i].wait_send()


def tp_sum(partial, collective_id, chunks=8):
    rows, width = partial.shape
    piece = (chunks, rows // chunks // 2, width)
    return pl.pallas_call(
        functools.partial(tp_sum_body, chunks),
        out_shape=shaped(partial.shape, partial.dtype),
        in_specs=[pl.BlockSpec(memory_space=pltpu.VMEM)],
        out_specs=pl.BlockSpec(memory_space=pltpu.VMEM),
        scratch_shapes=[
            pltpu.VMEM(piece, partial.dtype),
            pltpu.VMEM(piece, partial.dtype),
            pltpu.VMEM(piece, partial.dtype),
            pltpu.SemaphoreType.DMA((3, chunks)),
            pltpu.SemaphoreType.DMA((3, chunks)),
        ],
        compiler_params=params(collective_id=collective_id, has_side_effects=True),
    )(partial)


def per_device(
    tokens_in, query_weight, key_weight, value_weight, output_projection_matrix, gate_weight, up_weight,
    down_projection_matrix, gain_attn, gain_ffn, query_in, query_out, key_in, key_out, value_in, value_out,
    output_in, output_adapter_second, gate_in, gate_out, up_in, up_out, down_in, down_adapter_second,
    adapter_index, cotangent,
):
    seqs, rows, width = tokens_in.shape
    n = lax.axis_size("ctx")
    shards = lax.axis_size("tp")
    me_ctx = lax.axis_index("ctx")
    me_tp = lax.axis_index("tp")
    tables = query_in.shape[0]
    rank = query_in.shape[2]
    q_width = query_weight.shape[1]
    kv_width = key_weight.shape[1]
    heads = q_width // HEAD_DIM
    ff = gate_weight.shape[1]
    all_width = q_width + 2 * kv_width

    w_first = lax.all_gather(
        jnp.concatenate([query_weight, key_weight, value_weight], axis=1), "ctx", axis=0, tiled=True
    )
    w_out = lax.all_gather(output_projection_matrix, "ctx", axis=1, tiled=True)
    w_gate = lax.all_gather(gate_weight, "ctx", axis=0, tiled=True)
    w_up = lax.all_gather(up_weight, "ctx", axis=0, tiled=True)
    w_down = lax.all_gather(down_projection_matrix, "ctx", axis=1, tiled=True)

    def pick(table):
        return jnp.stack([lax.dynamic_index_in_dim(table, adapter_index[s], 0, False) for s in range(seqs)])

    def first(*picked):
        joined = jnp.concatenate([pick(item) for item in picked], axis=2)
        return jnp.pad(joined, ((0, 0), (0, 0), (0, LORA - joined.shape[2])))

    def second(table, at):
        item = pick(table) * jnp.asarray(adapter_scale, bf16)
        return jnp.pad(item, ((0, 0), (at, LORA - at - rank), (0, 0)))

    a_first = first(query_in, key_in, value_in)
    b_first = jnp.concatenate(
        [second(query_out, 0), second(key_out, rank), second(value_out, 2 * rank)], axis=2
    )
    a_gu = first(gate_in, up_in)
    b_gate = second(gate_out, 0)
    b_up = second(up_out, rank)
    a_out = first(output_in)
    b_out = second(output_adapter_second, 0)
    a_down = first(down_in)
    b_down = second(down_adapter_second, 0)
    gain_one = gain_attn.astype(f32)[None, :]
    gain_two = gain_ffn.astype(f32)[None, :]

    lane = jnp.arange(HEAD_DIM)
    frequency = theta_base ** (-((lane % (HEAD_DIM // 2)).astype(f32) * 2.0 / HEAD_DIM))
    position = (me_ctx * rows + jnp.arange(rows, dtype=jnp.int32)).astype(f32)
    angles = position[:, None] * frequency[None, :]
    cosine = jnp.cos(angles)
    sine = jnp.where(lane < HEAD_DIM // 2, -1.0, 1.0)[None, :] * jnp.sin(angles)
    shrink = HEAD_DIM ** (-0.5)
    ones = jnp.ones((rows, kv_width), f32)
    cos_kv = jnp.concatenate([cosine, ones], axis=1)
    sin_kv = jnp.concatenate([sine, jnp.zeros_like(ones)], axis=1)
    cos_q = jnp.tile(cosine * shrink, (1, 2))
    sin_q = jnp.tile(sine * shrink, (1, 2))
    cos_all = jnp.concatenate([jnp.tile(cos_q, (1, heads // 2)), cos_kv], axis=1)
    sin_all = jnp.concatenate([jnp.tile(sin_q, (1, heads // 2)), sin_kv], axis=1)
    place = me_ctx.astype(jnp.int32).reshape(1)

    def call(body, ins, outs, scratch=(), scalars=(), flops=0, limit=60):
        specs = [item[1] for item in ins]
        args = [item[0] for item in ins]
        moved = sum(a.size * a.dtype.itemsize for a in args)
        return pl.pallas_call(
            body,
            out_shape=[shaped(shape, dtype) for shape, dtype, _ in outs],
            grid_spec=pltpu.PrefetchScalarGridSpec(
                num_scalar_prefetch=len(scalars),
                grid=(seqs,),
                in_specs=specs,
                out_specs=[spec for _, _, spec in outs],
                scratch_shapes=list(scratch),
            ),
            cost_estimate=pl.CostEstimate(flops=flops, bytes_accessed=moved, transcendentals=0),
            compiler_params=params(limit, dimension_semantics=("arbitrary",)),
            name=body.__name__,
        )(*scalars, *args)

    row = per_seq(rows, width)
    pay = per_seq(rows, width + LORA)
    total_rows = seqs * rows

    q, kv, xn_one, s_one = call(
        qkv_body,
        [
            (tokens_in, row), (gain_one, whole(1, width)), (w_first, whole(width, all_width)),
            (a_first, per_seq(width, LORA)), (b_first, per_seq(LORA, all_width)),
            (cos_all, whole(rows, all_width)), (sin_all, whole(rows, all_width)),
        ],
        [
            ((seqs, rows, q_width), bf16, per_seq(rows, q_width)),
            ((seqs, rows, 2 * kv_width), bf16, per_seq(rows, 2 * kv_width)),
            ((seqs, rows, width), bf16, row),
            ((seqs, rows, LORA), bf16, per_seq(rows, LORA)),
        ],
        flops=2 * total_rows * width * (all_width + LORA),
    )
    kv_all = ring_gather(kv, n, 1)
    kv_spec = pl.BlockSpec((n, None, rows, 2 * kv_width), lambda s, *_: (0, s, 0, 0))
    stat = per_seq(heads, rows)
    ob, lse = call(
        attn_fwd_body,
        [(q, per_seq(rows, q_width)), (kv_all, kv_spec)],
        [((seqs, rows, q_width), bf16, per_seq(rows, q_width)), ((seqs, heads, rows), f32, stat)],
        scratch=[
            pltpu.VMEM((heads, HEAD_DIM, rows), f32),
            pltpu.VMEM((heads, rows), f32),
            pltpu.VMEM((heads, rows), f32),
        ],
        scalars=(place,),
        flops=4 * total_rows * q_width * rows * n,
    )
    (p1,) = call(
        mix_body,
        [(ob, per_seq(rows, q_width)), (w_out, whole(q_width, width)), (a_out, per_seq(q_width, LORA))],
        [((seqs, rows, width + LORA), bf16, pay)],
        flops=2 * total_rows * q_width * width,
    )
    z = tp_sum(p1.reshape(total_rows, -1), 2).reshape(p1.shape)
    b_out_item = (b_out, per_seq(LORA, width))
    p2, p3, dbg, dbu, dad = call(
        ffn_body,
        [
            (tokens_in, row), (z, pay), b_out_item, (gain_two, whole(1, width)),
            (a_gu, per_seq(width, LORA)), (w_gate, whole(width, ff)), (w_up, whole(width, ff)),
            (b_gate, per_seq(LORA, ff)), (b_up, per_seq(LORA, ff)), (w_down, whole(ff, width)),
            (a_down, per_seq(ff, LORA)), (b_down, per_seq(LORA, width)), (cotangent, row),
        ],
        [
            ((seqs, rows, width + LORA), bf16, pay), ((seqs, rows, width + LORA), bf16, pay),
            ((seqs, rank, ff), bf16, per_seq(rank, ff)), ((seqs, rank, ff), bf16, per_seq(rank, ff)),
            ((seqs, rank, ff), bf16, per_seq(rank, ff)),
        ],
        flops=12 * total_rows * width * ff,
    )
    p2 = tp_sum(p2.reshape(total_rows, -1), 2).reshape(p2.shape)
    dh, dob, dbo, dao, dgu = call(
        back_body,
        [
            (tokens_in, row), (z, pay), b_out_item, (gain_two, whole(1, width)),
            (a_gu, per_seq(width, LORA)), (p2, pay), (cotangent, row), (w_out, whole(q_width, width)),
            (a_out, per_seq(q_width, LORA)), (ob, per_seq(rows, q_width)),
        ],
        [
            ((seqs, rows, width), bf16, row), ((seqs, rows, q_width), bf16, per_seq(rows, q_width)),
            ((seqs, rank, width), bf16, per_seq(rank, width)),
            ((seqs, rank, q_width), bf16, per_seq(rank, q_width)),
            ((seqs, 2 * rank, width), bf16, per_seq(2 * rank, width)),
        ],
        flops=2 * total_rows * q_width * width,
    )
    p3 = lax.psum(p3, "tp")

    def quarter(term):
        cut = term.reshape(seqs, -1, n, shards, width // n // shards)
        cut = lax.dynamic_index_in_dim(cut, me_tp, 3, False)
        return cut.reshape(seqs, -1, rank, width // shards).transpose(0, 2, 1, 3).reshape(seqs, rank, -1)

    early = jnp.concatenate([dbg, dbu, dad, dao, dbo, quarter(dgu)], axis=2)
    early = lax.psum(early, "ctx")

    dq, dkv = call(
        attn_bwd_body,
        [
            (q, per_seq(rows, q_width)), (kv_all, kv_spec), (dob, per_seq(rows, q_width)),
            (ob, per_seq(rows, q_width)), (lse, stat), (cos_q, whole(rows, 128)), (sin_q, whole(rows, 128)),
        ],
        [
            ((seqs, rows, q_width), bf16, per_seq(rows, q_width)),
            ((n, seqs, rows, 2 * kv_width), bf16, kv_spec),
        ],
        scratch=[pltpu.VMEM((heads, HEAD_DIM, rows), f32), pltpu.VMEM((heads, rows), f32)],
        scalars=(place,),
        flops=10 * total_rows * q_width * rows * n,
    )
    dkv = ring_scatter(dkv, n, 3)
    p4, dbf = call(
        dqkv_body,
        [
            (dq, per_seq(rows, q_width)), (dkv, per_seq(rows, 2 * kv_width)),
            (cos_kv, whole(rows, 2 * kv_width)), (sin_kv, whole(rows, 2 * kv_width)),
            (w_first, whole(width, all_width)), (b_first, per_seq(LORA, all_width)),
            (s_one, per_seq(rows, LORA)),
        ],
        [
            ((seqs, rows, width + LORA), bf16, pay),
            ((seqs, 3 * rank, all_width), bf16, per_seq(3 * rank, all_width)),
        ],
        flops=2 * total_rows * width * all_width,
    )
    p4 = tp_sum(p4.reshape(total_rows, -1), 2).reshape(p4.shape)
    result, dbd = call(
        result_body,
        [
            (tokens_in, row), (z, pay), b_out_item, (p3, pay), (b_down, per_seq(LORA, width)),
            (cotangent, row),
        ],
        [((seqs, rows, width), bf16, row), ((seqs, rank, width), bf16, per_seq(rank, width))],
    )
    grad_tokens, dfirst = call(
        last_body,
        [
            (tokens_in, row), (gain_one, whole(1, width)), (xn_one, row), (p4, pay),
            (a_first, per_seq(width, LORA)), (dh, row),
        ],
        [
            ((seqs, rows, width), bf16, row),
            ((seqs, 3 * rank, width), bf16, per_seq(3 * rank, width)),
        ],
    )
    dbq = dbf[:, :rank, :q_width]
    dbk = dbf[:, rank : 2 * rank, q_width : q_width + kv_width]
    dbv = dbf[:, 2 * rank :, q_width + kv_width :]
    late = jnp.concatenate([dbq, dbk, dbv, dbd, quarter(dfirst)], axis=2)
    late = lax.psum(late, "ctx")

    chooser = (
        adapter_index[:, None] == jnp.arange(tables, dtype=jnp.int32)[None, :]
    ).astype(f32)

    def collect(term):
        return jnp.sum(chooser[:, :, None, None] * term.astype(f32)[:, None], axis=0)

    def cuts(packed, sizes):
        out, at = [], 0
        for size in sizes:
            out.append(packed[:, :, at : at + size])
            at += size
        return out

    def own(term):
        part = width // n // shards
        return collect(lax.dynamic_slice_in_dim(term, me_ctx * part, part, 2)).transpose(0, 2, 1)

    quart = width // shards
    e = cuts(early, [ff, ff, ff, q_width, width, quart, quart])
    l = cuts(late, [q_width, kv_width, kv_width, width, quart, quart, quart])
    return (
        result,
        grad_tokens,
        own(l[4]),
        collect(l[0]),
        own(l[5]),
        collect(l[1]),
        own(l[6]),
        collect(l[2]),
        collect(e[3]).transpose(0, 2, 1),
        collect(e[4]),
        own(e[5]),
        collect(e[0]),
        own(e[6]),
        collect(e[1]),
        collect(e[2]).transpose(0, 2, 1),
        collect(l[3]),
    )


def solution(mesh):
    column = P(None, None, "tp")
    split = P(None, ("ctx", "tp"), None)
    return jax.shard_map(
        per_device,
        mesh=mesh,
        in_specs=(
            P(None, "ctx", None), P("ctx", "tp"), P("ctx", "tp"), P("ctx", "tp"), P("tp", "ctx"),
            P("ctx", "tp"), P("ctx", "tp"), P("tp", "ctx"), P(), P(), P(), column, P(), column, P(), column,
            P(None, "tp", None), P(), P(), column, P(), column, P(None, "tp", None), P(), P(),
            P(None, "ctx", None),
        ),
        out_specs=(
            P(None, "ctx", None), P(None, "ctx", None), split, column, split, column, split, column,
            P(None, "tp", None), P(), split, column, split, column, P(None, "tp", None), P(),
        ),
        check_vma=False,
    )
```

time: 1980 us -> 868 us (0.44)
  waiting for transfers between devices: 1320 us -> 318 us
  Pallas kernels: 0 us -> 464 us
  matrix products: 300 us -> 0 us
  blocking collectives: 123 us -> 0 us
  local copies, waits for them, and re-layouts: 156 us -> 36.2 us
  other arithmetic: 49.5 us -> 17.2 us
    unnamed x21 -> x7, waiting for transfers between devices: 531 us -> 2.48 us
    pallas_call x0 -> x14, Pallas kernels: none -> 464 us  [the longest x3 174 us: tp_sum(): pl.pallas_call(functools.partial(tp_sum_body, chunks), out_shape=shaped(p...]
    psum x4 -> x2, waiting for transfers between devices: 449 us -> 87.9 us  [the longest x1 87.9 us: per_device(): early = lax.psum(early, 'ctx')]
    dot_general x91 -> x0, matrix products: 300 us -> none  [the longest x5 42.4 us: project_back(): jnp.einsum('nao,nko->nak', reduced_gradient, selected_input_factor.astype...]
    unnamed x235 -> x63, local copies, waits for them, and re-layouts: 149 us -> 2.58 us
    all_gather x6 -> x5, waiting for transfers between devices: 299 us -> 227 us  [the longest x1 93.2 us: per_device(): w_down = lax.all_gather(down_projection_matrix, 'ctx', axis=1, tiled=True)]
    all_gather x2 -> x0, blocking collectives: 65.1 us -> none  [the longest x1 33.6 us: per_device(): lax.all_gather(key_weight, 'ctx', axis=0, tiled=True)]
    psum x3 -> x0, blocking collectives: 57.8 us -> none  [the longest x1 35.7 us: per_device(): lax.psum(collect(term_key_out).astype(jnp.bfloat16), 'ctx')]
  transfers between devices with their start and end apart: 16 -> 7, of which waited for: 15 -> 5; matrix products, arithmetic and copies ran while one was open for 18% -> 4% of each run, Pallas kernels for 0% -> 39%
where the time goes in v1:
time: 868 us; the launch traced here: 858 us
  Pallas kernels  464 us (53%)
  waiting for transfers between devices  318 us (37%)
  local copies, waits for them, and re-layouts  36.2 us (4%)
  between operations  22.8 us (3%)
  other arithmetic  17.2 us (2%)
    pallas_call x3, Pallas kernels, tp_sum(): pl.pallas_call(functools.partial(tp_sum_body, chunks), out_shape=shaped(p...  174 us
    pallas_call x9, Pallas kernels, call(): pl.pallas_call(body, out_shape=[shaped(shape, dtype) for shape, dtype, _...  157 us
    all_gather x1, waiting for transfers between devices, per_device(): w_down = lax.all_gather(down_projection_matrix, 'ctx', axis=1, tiled=True)  93.2 us
    all_gather x1, waiting for transfers between devices, per_device(): w_up = lax.all_gather(up_weight, 'ctx', axis=0, tiled=True)  92.5 us
    pallas_call x1, Pallas kernels, ring_scatter(): pl.pallas_call(functools.partial(ring_scatter_body, n), out_shape=shaped(...  89.5 us
    psum x1, waiting for transfers between devices, per_device(): early = lax.psum(early, 'ctx')  87.9 us
    pallas_call x1, Pallas kernels, ring_gather(): pl.pallas_call(functools.partial(ring_gather_body, n), out_shape=shaped((...  43.1 us
    all_gather x1, waiting for transfers between devices, per_device(): w_gate = lax.all_gather(gate_weight, 'ctx', axis=0, tiled=True)  22.2 us
  transfers between devices with their start and end apart: 7, of which 5 were waited for; matrix products, arithmetic and copies ran while one was open for 4% of the time, Pallas kernels for 39%

profile of v1, /device:TPU:0, one launch (start us, length us, event | category | flops | bytes accessed | tf_op | source)
XLA Modules:
  0.0 858.0 jit_solution(4652553761168666954)
XLA Ops:
  7.2 0.9 copy.128
  8.1 0.9 copy.129
  9.0 1.8 pad_maximum_fusion
  10.9 0.7 all-gather.8.cloned.1.call-update
  11.6 0.7 all-gather.10.cloned.1.call-update
  12.3 0.5 all-gather.12.cloned.1.call-update
  12.9 0.5 all-gather.14.cloned.1.call-update
  13.5 0.6 fusion.13
  22.1 1.1 copy.130
  23.2 1.2 broadcast_multiply_fusion
  24.8 1.0 copy.131
  26.0 0.5 copy-done.5
  26.8 0.6 broadcast_in_dim.28
  27.4 0.8 constant_dynamic-slice_fusion.31
  28.2 1.0 copy.135
  29.2 1.7 pad.45.a_ref
  30.9 0.9 pad.49.a_ref.ao_ref
  31.8 0.8 maximum_maximum_fusion.3
  32.7 1.9 copy.136
  34.6 1.7 pad.51.agu_ref
  36.5 1.6 pad.50.bo_ref
  38.1 1.6 pad.55.bd_ref
  39.8 0.8 copy.137
  40.6 1.4 pad.54.ad_ref
  42.2 1.2 pad.52.bg_ref
  43.4 1.2 pad.53.bu_ref
  44.6 0.6 broadcast_in_dim.29
  45.2 0.7 concatenate.38.cos_ref
  45.9 0.7 concatenate.39.sin_ref
  46.7 0.9 fusion.5.b_ref
  47.6 1.2 maximum_maximum_fusion.1
  48.8 19.3 %all-gather.6.cloned.1.call-done.w_ref = bf16[2048,640]{1,0:T(8,128)(2,1)} async-done(((bf16[256,640]{1,0:T(8,128)(2,1)}), bf16[2048,640]{1,0:T(8,128)(2,1)}) %all-gather.6.cloned.1.call-update) | async-done | bytes 2621456 | tf_op jit(solution)/shard_map/all_gather | solution.py:488
  68.1 11.4 %qkv_body.1 = (bf16[4,256,512]{2,1,0:T(8,128)(2,1)}, bf16[4,256,128]{2,1,0:T(8,128)(2,1)}, bf16[4,256,2048]{2,1,0:T(8,128)(2,1)}, bf16[4,256,128]{2,1,0:T(8,128)(2,1)}) custom-call(bf16[4,256,2048]{2,1,0:T(8,128)(2,1)} %t_ref.9, f32[1,2048]{1,0:T(1,128)} %bitcast.65, bf16[2048,640]{1,0:T(8,128)(2,1)} %all-gather.6.cloned.1.call-done.w_ref, ...), custom_call_target="tpu_custom_call" | custom-call | flops 3221225472 | bytes 10887168 | tf_op jit(solution)/shard_map/qkv_body/pallas_call | solution.py:541
  79.4 43.1 %shard_map.369.kv_ref = bf16[8,4,256,128]{3,2,1,0:T(8,128)(2,1)} custom-call(bf16[4,256,128]{2,1,0:T(8,128)(2,1)} %get-tuple-element.41.in_ref), custom_call_target="tpu_custom_call" | custom-call | tf_op jit(solution)/shard_map/pallas_call | solution.py:343
  122.6 12.3 %attn_fwd_body.1 = (bf16[4,256,512]{2,1,0:T(8,128)(2,1)}, f32[4,8,256]{2,1,0:T(8,128)}) custom-call(s32[1]{0:T(128)} %bitcast.c_ref, bf16[4,256,512]{2,1,0:T(8,128)(2,1)} %get-tuple-element.40.q_ref, bf16[8,4,256,128]{3,2,1,0:T(8,128)(2,1)} %shard_map.369.kv_ref), custom_call_target="tpu_custom_call" | custom-call | flops 4294967296 | bytes 3145728 | tf_op jit(solution)/shard_map/attn_fwd_body/pallas_call | solution.py:541
  134.9 6.7 mix_body.1
  141.6 58.3 %shard_map.370 = bf16[1024,2176]{1,0:T(8,128)(2,1)} custom-call(bf16[1024,2176]{1,0:T(8,128)(2,1)} %bitcast.45), custom_call_target="tpu_custom_call" | custom-call | tf_op jit(solution)/shard_map/pallas_call | solution.py:453
  199.9 22.2 %all-gather.10.cloned.1.call-done.wg_ref = bf16[2048,1408]{1,0:T(8,128)(2,1)} async-done(((bf16[256,1408]{1,0:T(8,128)(2,1)}), bf16[2048,1408]{1,0:T(8,128)(2,1)}) %all-gather.10.cloned.1.call-update) | async-done | bytes 5767184 | tf_op jit(solution)/shard_map/all_gather | solution.py:492
  222.1 92.5 %all-gather.12.cloned.1.call-done.wu_ref = bf16[2048,1408]{1,0:T(8,128)(2,1)} async-done(((bf16[256,1408]{1,0:T(8,128)(2,1)}), bf16[2048,1408]{1,0:T(8,128)(2,1)}) %all-gather.12.cloned.1.call-update) | async-done | bytes 5767184 | tf_op jit(solution)/shard_map/all_gather | solution.py:493
  314.6 93.2 %all-gather.14.cloned.1.call-done.wd_ref = bf16[1408,2048]{1,0:T(8,128)(2,1)} async-done(((bf16[1408,256]{1,0:T(8,128)(2,1)}), bf16[1408,2048]{1,0:T(8,128)(2,1)}) %all-gather.14.cloned.1.call-update) | async-done | bytes 5767184 | tf_op jit(solution)/shard_map/all_gather | solution.py:494
  407.9 63.3 %ffn_body.1 = (bf16[4,256,2176]{2,1,0:T(8,128)(2,1)}, bf16[4,256,2176]{2,1,0:T(8,128)(2,1)}, bf16[4,16,1408]{2,1,0:T(8,128)(2,1)}, bf16[4,16,1408]{2,1,0:T(8,128)(2,1)}, bf16[4,16,1408]{2,1,0:T(8,128)(2,1)}) custom-call(bf16[4,256,2048]{2,1,0:T(8,128)(2,1)} %t_ref.9, bf16[4,256,2176]{2,1,0:T(8,128)(2,1)} %bitcast.40, bf16[4,128,2048]{2,1,0:T(8,128)(2,1)} %pad.50.bo_ref, ...), custom_call_target="tpu_custom_call" | custom-call | flops 35433480192 | bytes 40771584 | tf_op jit(solution)/shard_map/ffn_body/pallas_call | solution.py:541
  471.2 58.3 %shard_map.371 = bf16[1024,2176]{1,0:T(8,128)(2,1)} custom-call(bf16[1024,2176]{1,0:T(8,128)(2,1)} %bitcast.46), custom_call_target="tpu_custom_call" | custom-call | tf_op jit(solution)/shard_map/pallas_call | solution.py:453
  529.6 18.6 %back_body.1 = (bf16[4,256,2048]{2,1,0:T(8,128)(2,1)}, bf16[4,256,512]{2,1,0:T(8,128)(2,1)}, bf16[4,16,2048]{2,1,0:T(8,128)(2,1)}, bf16[4,16,512]{2,1,0:T(8,128)(2,1)}, bf16[4,32,2048]{2,1,0:T(8,128)(2,1)}) custom-call(bf16[4,256,2048]{2,1,0:T(8,128)(2,1)} %t_ref.9, bf16[4,256,2176]{2,1,0:T(8,128)(2,1)} %bitcast.41, bf16[4,128,2048]{2,1,0:T(8,128)(2,1)} %pad.50.bo_ref, ...), custom_call_target="tpu_custom_call" | custom-call | flops 2147483648 | bytes 25174016 | tf_op jit(solution)/shard_map/back_body/pallas_call | solution.py:541
  548.2 14.7 %attn_bwd_body.1 = (bf16[4,256,512]{2,1,0:T(8,128)(2,1)}, bf16[8,4,256,128]{3,2,1,0:T(8,128)(2,1)}) custom-call(s32[1]{0:T(128)} %bitcast.c_ref, bf16[4,256,512]{2,1,0:T(8,128)(2,1)} %get-tuple-element.40.q_ref, bf16[8,4,256,128]{3,2,1,0:T(8,128)(2,1)} %shard_map.369.kv_ref, bf16[4,256,512]{2,1,0:T(8,128)(2,1)} %get-tuple-element.47.do_ref, ...), custom_call_target="tpu_custom_call" | custom-call | flops 10737418240 | bytes 5537792 | tf_op jit(solution)/shard_map/attn_bwd_body/pallas_call | solution.py:541
  562.9 89.5 %shard_map.372.dkv_ref = f32[4,256,128]{2,1,0:T(8,128)} custom-call(bf16[8,4,256,128]{3,2,1,0:T(8,128)(2,1)} %get-tuple-element.50.in_ref), custom_call_target="tpu_custom_call" | custom-call | tf_op jit(solution)/shard_map/pallas_call | solution.py:399
  652.3 8.2 dqkv_body.1
  660.6 57.7 %shard_map.373 = bf16[1024,2176]{1,0:T(8,128)(2,1)} custom-call(bf16[1024,2176]{1,0:T(8,128)(2,1)} %bitcast.47), custom_call_target="tpu_custom_call" | custom-call | tf_op jit(solution)/shard_map/pallas_call | solution.py:453
  718.3 11.5 %last_body.1 = (bf16[4,256,2048]{2,1,0:T(8,128)(2,1)}, bf16[4,48,2048]{2,1,0:T(8,128)(2,1)}) custom-call(bf16[4,256,2048]{2,1,0:T(8,128)(2,1)} %t_ref.9, f32[1,2048]{1,0:T(1,128)} %bitcast.66, bf16[4,256,2048]{2,1,0:T(8,128)(2,1)} %get-tuple-element.45.xn_ref, bf16[4,256,2176]{2,1,0:T(8,128)(2,1)} %bitcast.44, bf16[4,2048,128]{2,1,0:T(8,128)(2,1)} %pad.45.a_ref, ...), custom_call_target="tpu_custom_call" | custom-call | bytes 19144704 | tf_op jit(solution)/shard_map/last_body/pallas_call | solution.py:541
  729.7 3.6 reshape.227
  733.3 2.5 dynamic-slice_reduce_fusion
  736.1 0.9 slice.46
  737.0 1.1 reshape.230
  738.1 1.7 dynamic-slice_reduce_fusion.1
  740.2 0.9 fusion.12
  741.1 10.4 %result_body.1 = (bf16[4,256,2048]{2,1,0:T(8,128)(2,1)}, bf16[4,16,2048]{2,1,0:T(8,128)(2,1)}) custom-call(bf16[4,256,2048]{2,1,0:T(8,128)(2,1)} %t_ref.9, bf16[4,256,2176]{2,1,0:T(8,128)(2,1)} %bitcast.42, bf16[4,128,2048]{2,1,0:T(8,128)(2,1)} %pad.50.bo_ref, bf16[4,256,2176]{2,1,0:T(8,128)(2,1)} %all-reduce.17.cloned.1.call-done.p3_ref, ...), custom_call_target="tpu_custom_call" | custom-call | bytes 21495808 | tf_op jit(solution)/shard_map/result_body/pallas_call | solution.py:541
  751.5 1.8 concatenate.40
  753.4 87.9 %all-reduce.19.cloned.1.call-done = (bf16[4,16,7808]{2,1,0:T(8,128)(2,1)}, bf16[4,16,4224]{2,1,0:T(8,128)(2,1)}) async-done(((bf16[4,16,7808]{2,1,0:T(8,128)(2,1)}, bf16[4,16,4224]{2,1,0:T(8,128)(2,1)}), (bf16[4,16,7808]{2,1,0:T(8,128)(2,1)}, bf16[4,16,4224]{2,1,0:T(8,128)(2,1)})) %all-reduce.19.cloned.1.call-update) | async-done | bytes 1540112 | tf_op jit(solution)/shard_map/psum | solution.py:637
  841.2 1.2 slice_convert_fusion.4
  842.5 1.0 slice_convert_fusion.1
  843.6 0.9 slice_convert_fusion.5
  845.0 1.9 multiply_reduce_fusion
  846.9 1.0 multiply_reduce_fusion.5
  847.9 2.0 multiply_reduce_fusion.2
  849.9 1.0 multiply_reduce_fusion.7
  (118 shorter events, 2.9 us)
Async XLA Ops:
  7.2 60.9 %all-gather.6.cloned.1.call-start = ((), (), s32[]{:S(2)}) async-start(), calls=%async_computation | async-start | bytes 2949120 | tf_op jit(solution)/shard_map/all_gather | solution.py:488
  9.0 4.5 copy-start.22
  10.8 11.1 %copy-start.10 = (bf16[8,2048,16]{1,2,0:T(8,128)(2,1)S(1)}, bf16[8,2048,16]{1,2,0:T(8,128)(2,1)}, u32[]{:S(2)}) copy-start(bf16[8,2048,16]{1,2,0:T(8,128)(2,1)} %param.36) | copy-start | bytes 1572868
  10.8 11.2 %copy-start.11 = (bf16[8,2048,16]{1,2,0:T(8,128)(2,1)S(1)}, bf16[8,2048,16]{1,2,0:T(8,128)(2,1)}, u32[]{:S(2)}) copy-start(bf16[8,2048,16]{1,2,0:T(8,128)(2,1)} %param.40) | copy-start | bytes 1572868
  10.8 11.1 %copy-start.12 = (bf16[8,2048,16]{1,2,0:T(8,128)(2,1)S(1)}, bf16[8,2048,16]{1,2,0:T(8,128)(2,1)}, u32[]{:S(2)}) copy-start(bf16[8,2048,16]{1,2,0:T(8,128)(2,1)} %param.38) | copy-start | bytes 1572868
  10.8 124.1 %all-gather.8.cloned.1.call-start = ((), (), s32[]{:S(2)}) async-start(), calls=%async_computation.1 | async-start | bytes 2359296 | tf_op jit(solution)/shard_map/all_gather | solution.py:491
  11.6 210.5 %all-gather.10.cloned.1.call-start = ((), (), s32[]{:S(2)}) async-start(), calls=%async_computation.2 | async-start | bytes 6488064 | tf_op jit(solution)/shard_map/all_gather | solution.py:492
  12.3 302.3 %all-gather.12.cloned.1.call-start = ((), (), s32[]{:S(2)}) async-start(), calls=%async_computation.3 | async-start | bytes 6488064 | tf_op jit(solution)/shard_map/all_gather | solution.py:493
  12.9 395.0 %all-gather.14.cloned.1.call-start = ((), (), s32[]{:S(2)}) async-start(), calls=%async_computation.4 | async-start | bytes 6488064 | tf_op jit(solution)/shard_map/all_gather | solution.py:494
  13.5 727.6 %all-reduce.17.cloned.1.call-start = ((), (), s32[]{:S(2)}) async-start(), calls=%async_computation.5 | async-start | bytes 8912896 | tf_op jit(solution)/shard_map/psum | solution.py:629
  24.6 2.0 copy-start.4
  24.7 2.0 copy-start.25
  25.9 0.7 copy-start.5
  29.2 1.7 copy-start
  29.2 2.6 copy-start.13
  29.2 2.6 copy-start.14
  34.6 1.8 copy-start.15
  34.6 1.7 copy-start.16
  38.1 1.7 copy-start.17
  40.6 1.5 copy-start.18
  40.6 1.4 copy-start.19
  42.1 2.5 copy-start.26
  43.3 3.2 copy-start.23
  43.3 3.2 copy-start.24
  43.3 3.3 copy-start.21
  529.5 311.7 %all-reduce.19.cloned.1.call-start = ((), (), s32[]{:S(2)}) async-start(), calls=%async_computation.6 | async-start | bytes 3080192 | tf_op jit(solution)/shard_map/psum | solution.py:637
  733.3 3.7 copy-start.3
  736.1 3.9 copy-start.9
  737.0 3.1 copy-start.8
  737.0 3.1 copy-start.7
  738.1 2.0 copy-start.20
  738.1 2.0 copy-start.6
  740.2 11.3 %copy-start.1 = (bf16[4,16,7808]{2,1,0:T(8,128)(2,1)}, bf16[4,16,7808]{2,1,0:T(8,128)(2,1)S(1)}, u32[]{:S(2)}) copy-start(bf16[4,16,7808]{2,1,0:T(8,128)(2,1)S(1)} %constant_dynamic-update-slice_fusion) | copy-start | bytes 2998276
  841.2 2.2 copy-start.2
Sparse Core Ops, SparseCore 0:
  10.9 57.1 all-gather.5
  70.1 57.0 all-gather.7
  129.4 92.6 all-gather.9
  224.1 90.4 all-gather.11
  316.5 91.2 all-gather.13
  529.6 87.5 all-reduce.16
  753.4 87.7 all-reduce.18
